TPU v7x, 128 devices: a whole 4x4x4 slice. The times are simulated.
128 devices in a mesh: ctx: 32 (over z, x, core), exp: 4 (over y).
Axes of the slice: x: 4, y: 4, z: 4, core: 2. Of those that a mesh axis runs over, the one named last changes fastest.
Arguments:
- residual: bfloat16 [16384, 2048], P(('ctx', 'exp')), may hold values from -6 to 6
- mixed_qkv: bfloat16 [16384, 4096], P(('ctx', 'exp')), may hold values from -6 to 6
- output_gate: bfloat16 [16384, 2048], P(('ctx', 'exp')), may hold values from -6 to 6
- log_decay: float32 [16384, 16], P(('ctx', 'exp')), may hold values from -0.8 to 0, as said below
- write_strength: float32 [16384, 16], P(('ctx', 'exp')), may hold values from 0 to 1, as said below
- conv_weight: float32 [4, 4096], replicated, may hold values from -3 to 3
- norm_gain: float32 [128], replicated, may hold values from 0.1 to 1.9
- out_weight: bfloat16 [2048, 2048], P(None, 'exp'), may hold values from -0.125 to 0.125
- post_gain: float32 [2048], replicated, may hold values from 0.1 to 1.9
- router_weight: bfloat16 [2048, 256], replicated, may hold values from -0.125 to 0.125
- expert_ids: int32 [16384, 10], P(('ctx', 'exp')), may hold values from 0 to 255, all different within a row; in each aligned block of 128 rows (0 to 127, 128 to 255, ...) at most 6 rows name the same one
- expert_gate: bfloat16 [256, 2048, 512], P(('ctx', 'exp')), may hold values from -0.125 to 0.125
- expert_up: bfloat16 [256, 2048, 512], P(('ctx', 'exp')), may hold values from -0.125 to 0.125
- expert_down: bfloat16 [256, 512, 2048], P(('ctx', 'exp')), may hold values from -0.25 to 0.25
- shared_gate: bfloat16 [2048, 512], replicated, may hold values from -0.125 to 0.125
- shared_up: bfloat16 [2048, 512], replicated, may hold values from -0.125 to 0.125
- shared_down: bfloat16 [512, 2048], replicated, may hold values from -0.25 to 0.25
- shared_switch: bfloat16 [2048], replicated, may hold values from -0.125 to 0.125
Outputs:
- layer_out: bfloat16 [16384, 2048], P(('ctx', 'exp'))
Inputs may be any that keep to these rules, and one draw needn't show every extreme that they name: `expert_ids`: in the 128 rows of one device no expert is named more than 6 times. `log_decay`: negative. `write_strength`: positive.
All inputs are finite; a program needn't handle non-finite values.
Results may differ from a plain program's by a relative error of at most 0.011.
Values may be sent and summed in bfloat16 or wider, within the bound.
A program may use at most 128 MiB of HBM per device.

v0:
```python
import jax
import jax.numpy as jnp
from jax import lax
from jax.sharding import Mesh
from jax.sharding import PartitionSpec as P

VHEADS = 16
KHEADS = 8
HEAD = 128
TOP = 10
SPAN = 64
CTX_EXP = ("ctx_0", "ctx_1", "ctx_2", "exp")
CTX = ("ctx_0", "ctx_1", "ctx_2")


highest_precision = lax.Precision.HIGHEST
epsilon = 1e-06


def passed_along(value, axis, steps):
    count = lax.axis_size(axis)
    first, last = (max(0, -steps), min(count, count - steps))
    return lax.ppermute(value, axis, [(source, source + steps) for source in range(first, last)])


def sent_together(arrays, axis, split_dim, concat_dim, along):
    ends, at = ([], 0)
    for a in arrays[:-1]:
        at += a.shape[along]
        ends.append(at)
    both = jnp.concatenate(arrays, axis=along)
    return tuple(
        jnp.split(
            lax.all_to_all(both, axis, split_axis=split_dim, concat_axis=concat_dim, tiled=True),
            ends,
            axis=along,
        )
    )


def nothing_yet(x, identity):
    return jax.tree.map(
        lambda part, zero: jnp.zeros_like(part) + jnp.asarray(zero, part.dtype), x, identity
    )


def entering(x, axes, combine, identity):
    before = start = nothing_yet(x, identity)
    subtotal = x
    for axis in reversed(axes):
        peers, index = (lax.axis_size(axis), lax.axis_index(axis))
        pieces = jax.tree.map(lambda part: lax.all_gather(part, axis), subtotal)
        inside, subtotal = (start, start)
        for k in range(peers):
            passed = k < index
            subtotal = combine(subtotal, jax.tree.map(lambda part: part[k], pieces))
            inside = jax.tree.map(lambda new, old: jnp.where(passed, new, old), subtotal, inside)
        before = combine(inside, before)
    return before


def in_order(blocks, dim):
    shape = list(blocks.shape[1:])
    shape[dim] *= blocks.shape[0]
    return jnp.moveaxis(blocks, 0, dim).reshape(shape)


def from_everyone(x, axis):
    copies = jnp.broadcast_to(x, (lax.axis_size(axis), *x.shape))
    return lax.all_to_all(copies, axis, split_axis=0, concat_axis=0, tiled=True)


def gathered_copies(x, axis, dim):
    return in_order(from_everyone(x, axis), dim)


def grouped_exchange(x, axis, split_dim, concat_dim, work, item_dim, out_dim):
    items = jax.tree.leaves(x)[0].shape[item_dim]
    count = 2 if items % 2 == 0 else 1
    gathered = []
    for k in range(count):
        group = jax.tree.map(
            lambda a: lax.slice_in_dim(
                a, k * (items // count), (k + 1) * (items // count), axis=item_dim
            ),
            x,
        )
        gathered.append(
            work(
                lax.all_to_all(
                    group, axis, split_axis=split_dim, concat_axis=concat_dim, tiled=True
                )
            )
        )
    return jax.tree.map(lambda *parts: jnp.concatenate(parts, axis=out_dim), *gathered)


def short_conv(mixed_qkv, conv_weight, before):
    row_count = mixed_qkv.shape[0]
    padded = jnp.concatenate([before, mixed_qkv], axis=0).astype(jnp.float32)
    summed = conv_weight[3] * padded[3 : 3 + row_count]
    for tap_index in range(3):
        summed = summed + conv_weight[tap_index] * padded[tap_index : tap_index + row_count]
    return jax.nn.silu(summed)


def unit_rows(values_in):
    return values_in * lax.rsqrt(jnp.sum(values_in * values_in, axis=-1, keepdims=True) + epsilon)


def prepare(mixed_qkv, conv_weight, before):
    activated = short_conv(mixed_qkv, conv_weight, before)
    row_count = activated.shape[0]
    key_width = KHEADS * HEAD
    query_rows = unit_rows(activated[:, :key_width].reshape(row_count, KHEADS, HEAD)) * HEAD ** (
        -0.5
    )
    key_rows = unit_rows(activated[:, key_width : 2 * key_width].reshape(row_count, KHEADS, HEAD))
    value_rows = activated[:, 2 * key_width :].reshape(row_count, VHEADS, HEAD)
    per_group = VHEADS // KHEADS
    query_rows = jnp.repeat(query_rows, per_group, axis=1)
    key_rows = jnp.repeat(key_rows, per_group, axis=1)
    return (
        query_rows.transpose(1, 0, 2),
        key_rows.transpose(1, 0, 2),
        value_rows.transpose(1, 0, 2),
    )


def to_spans(head_rows):
    head_count, row_count, inner_width = head_rows.shape
    return head_rows.reshape(head_count, row_count // SPAN, SPAN, inner_width).transpose(1, 0, 2, 3)


def rates_to_spans(token_rates):
    row_count, head_count = token_rates.shape
    return token_rates.T.reshape(head_count, row_count // SPAN, SPAN).transpose(1, 0, 2)


def span_terms(query_rows, key_rows, value_rows, decay_rows, strength_rows):
    length = query_rows.shape[1]
    inner_width = key_rows.shape[2]
    cumul = jnp.cumsum(decay_rows, axis=1)
    causal = (
        jnp.arange(length, dtype=jnp.int32)[:, None] >= jnp.arange(length, dtype=jnp.int32)[None, :]
    )
    strict = (
        jnp.arange(length, dtype=jnp.int32)[:, None] > jnp.arange(length, dtype=jnp.int32)[None, :]
    )
    log_gap = cumul[:, :, None] - cumul[:, None, :]
    ratios = jnp.where(causal, jnp.exp(jnp.where(causal, log_gap, 0.0)), 0.0)
    key_inner = jnp.einsum("hck,hsk->hcs", key_rows, key_rows, precision=highest_precision)
    lower_part = jnp.where(strict, ratios * key_inner, 0.0) * strength_rows[:, :, None]
    system = jnp.eye(length, dtype=jnp.float32)[None] + lower_part
    decays = jnp.exp(cumul)
    right_operand = jnp.concatenate(
        [
            strength_rows[:, :, None] * decays[:, :, None] * key_rows,
            strength_rows[:, :, None] * value_rows,
        ],
        axis=2,
    )
    solved = jax.scipy.linalg.solve_triangular(
        system, right_operand, lower=True, unit_diagonal=True
    )
    key_weights = solved[:, :, :inner_width]
    fresh_values = solved[:, :, inner_width:]
    to_end = jnp.exp(cumul[:, -1:] - cumul)
    decayed_state = key_rows * to_end[:, :, None]
    identity = jnp.eye(inner_width, dtype=jnp.float32)[None]
    carry_transform = jnp.exp(cumul[:, -1])[:, None, None] * identity - jnp.einsum(
        "hck,hcj->hkj", decayed_state, key_weights, precision=highest_precision
    )
    carry_offset = jnp.einsum(
        "nae,nap->nep", decayed_state, fresh_values, precision=highest_precision
    )
    scores = jnp.einsum("hck,hsk->hcs", query_rows, key_rows, precision=highest_precision) * ratios
    read_transform = query_rows * decays[:, :, None] - jnp.einsum(
        "hcs,hsk->hck", scores, key_weights, precision=highest_precision
    )
    read_offset = jnp.einsum("hcs,hsv->hcv", scores, fresh_values, precision=highest_precision)
    return (carry_transform, carry_offset, read_transform, read_offset)


def apply_map(left_transform, right_operand):
    return jnp.einsum("coq,cqd->cod", left_transform, right_operand, precision=highest_precision)


def chain_pair(earlier, later):
    return (apply_map(later[0], earlier[0]), apply_map(later[0], earlier[1]) + later[1])


def run_experts(received, expert_gate, expert_up, expert_down):
    gate_part = jnp.einsum(
        "nesd,edf->nesf", received, expert_gate, preferred_element_type=jnp.float32
    )
    up_part = jnp.einsum("nesd,edf->nesf", received, expert_up, preferred_element_type=jnp.float32)
    expert_hidden = (jax.nn.silu(gate_part) * up_part).astype(jnp.bfloat16)
    return jnp.einsum(
        "nesf,efd->nesd", expert_hidden, expert_down, preferred_element_type=jnp.float32
    ).astype(jnp.bfloat16)


def local(
    residual,
    mixed_qkv,
    output_gate,
    log_decay,
    write_strength,
    conv_weight,
    norm_gain,
    out_weight,
    post_gain,
    router_weight,
    expert_ids,
    expert_gate,
    expert_up,
    expert_down,
    shared_gate,
    shared_up,
    shared_down,
    shared_switch,
):
    row_count = mixed_qkv.shape[0]
    model_width = residual.shape[1]
    before = passed_along(mixed_qkv[row_count - 3 :], CTX_EXP, 1)
    query_rows, key_rows, value_rows = prepare(mixed_qkv, conv_weight, before)
    span_parts = jax.vmap(span_terms)(
        to_spans(query_rows),
        to_spans(key_rows),
        to_spans(value_rows),
        rates_to_spans(log_decay),
        rates_to_spans(write_strength),
    )
    identity = jnp.broadcast_to(jnp.eye(HEAD, dtype=jnp.float32)[None], (VHEADS, HEAD, HEAD))
    zero_add = jnp.zeros((VHEADS, HEAD, HEAD), jnp.float32)

    def compose(carried, step_parts):
        return (chain_pair(carried, step_parts), None)

    (block_map, block_add), _ = lax.scan(
        compose, (identity, zero_add), (span_parts[0], span_parts[1])
    )
    exp_count = lax.axis_size("exp")
    share = VHEADS // exp_count
    member_map, member_add = sent_together(
        (
            block_map.reshape(exp_count, share, HEAD, HEAD),
            block_add.reshape(exp_count, share, HEAD, HEAD),
        ),
        "exp",
        0,
        0,
        1,
    )
    running = (identity[:share], zero_add[:share])
    prefixes = []
    for member in range(exp_count):
        prefixes.append(running)
        running = chain_pair(running, (member_map[member], member_add[member]))
    _, outer_add = entering(running, CTX, chain_pair, (identity[:share], zero_add[:share]))
    starts = jnp.stack([apply_map(prefix[0], outer_add) + prefix[1] for prefix in prefixes])
    start_state = lax.all_to_all(starts, "exp", split_axis=0, concat_axis=0, tiled=True).reshape(
        VHEADS, HEAD, HEAD
    )

    def emit_rows(current_state, step_parts):
        carry_transform, carry_offset, read_transform, read_offset = step_parts
        produced_output = (
            jnp.einsum("urm,umn->urn", read_transform, current_state, precision=highest_precision)
            + read_offset
        )
        return (apply_map(carry_transform, current_state) + carry_offset, produced_output)

    _, produced_output = lax.scan(emit_rows, start_state, span_parts)
    mixer_out = produced_output.transpose(0, 2, 1, 3).reshape(row_count, VHEADS, HEAD)
    gate_rows = output_gate.reshape(row_count, VHEADS, HEAD).astype(jnp.float32)
    normed = mixer_out * lax.rsqrt(
        jnp.mean(mixer_out * mixer_out, axis=-1, keepdims=True) + epsilon
    )
    normed = (
        (normed * norm_gain * jax.nn.silu(gate_rows))
        .reshape(row_count, VHEADS * HEAD)
        .astype(jnp.bfloat16)
    )
    column_blocks = jnp.dot(
        gathered_copies(normed, "exp", 0), out_weight, preferred_element_type=jnp.float32
    )
    projected = lax.all_to_all(column_blocks, "exp", split_axis=0, concat_axis=1, tiled=True)
    after_mix = (residual.astype(jnp.float32) + projected).astype(jnp.bfloat16)
    after_wide = after_mix.astype(jnp.float32)
    routed_in = (
        after_wide
        * lax.rsqrt(jnp.mean(after_wide * after_wide, axis=-1, keepdims=True) + epsilon)
        * post_gain
    ).astype(jnp.bfloat16)
    logits = jnp.dot(routed_in, router_weight, preferred_element_type=jnp.float32)
    chosen = jnp.exp(jnp.take_along_axis(logits, expert_ids, axis=1))
    gate_weights = chosen / jnp.sum(chosen, axis=1, keepdims=True)
    ctx_count = lax.axis_size(CTX)
    devices = ctx_count * exp_count
    local_count = expert_gate.shape[0]
    experts_total = local_count * devices
    capacity = row_count * TOP * 6 // (experts_total * 5)
    flat_ids = expert_ids.reshape(-1)
    onehot = (flat_ids[:, None] == jnp.arange(experts_total, dtype=jnp.int32)[None, :]).astype(
        jnp.int32
    )
    slot_rank = jnp.sum((jnp.cumsum(onehot, axis=0) - onehot) * onehot, axis=1)
    token_of = jnp.arange(row_count * TOP, dtype=jnp.int32) // TOP
    outgoing = (
        jnp.zeros((experts_total, capacity, model_width), jnp.bfloat16)
        .at[flat_ids, slot_rank]
        .set(routed_in[token_of])
    )
    shared_hidden = (
        jax.nn.silu(jnp.dot(routed_in, shared_gate, preferred_element_type=jnp.float32))
        * jnp.dot(routed_in, shared_up, preferred_element_type=jnp.float32)
    ).astype(jnp.bfloat16)
    switch_rows = jax.nn.sigmoid(
        jnp.dot(routed_in, shared_switch, preferred_element_type=jnp.float32)
    )
    shared_out = switch_rows[:, None] * jnp.dot(
        shared_hidden, shared_down, preferred_element_type=jnp.float32
    )

    def serve_slots(received):
        result = run_experts(received, expert_gate, expert_up, expert_down)
        return lax.all_to_all(result, CTX_EXP, split_axis=0, concat_axis=0, tiled=True)

    returned = grouped_exchange(
        outgoing.reshape(devices, local_count, capacity, model_width),
        CTX_EXP,
        0,
        0,
        serve_slots,
        2,
        2,
    )
    returned = returned.reshape(experts_total, capacity, model_width)
    pulled = returned[flat_ids, slot_rank].reshape(row_count, TOP, model_width)
    routed = jnp.sum(pulled.astype(jnp.float32) * gate_weights[:, :, None], axis=1)
    return (after_wide + routed + shared_out).astype(jnp.bfloat16)


def solution(mesh):
    finer = Mesh(
        mesh.devices.reshape(4, 4, 2, mesh.shape["exp"]), ("ctx_0", "ctx_1", "ctx_2", "exp")
    )
    placed = (
        P(CTX_EXP, None),
        P(CTX_EXP, None),
        P(CTX_EXP, None),
        P(CTX_EXP, None),
        P(CTX_EXP, None),
        P(),
        P(),
        P(None, "exp"),
        P(),
        P(),
        P(CTX_EXP, None),
        P(CTX_EXP, None, None),
        P(CTX_EXP, None, None),
        P(CTX_EXP, None, None),
        P(),
        P(),
        P(),
        P(),
    )
    return jax.shard_map(
        local, mesh=finer, in_specs=placed, out_specs=P(CTX_EXP, None), check_vma=False
    )
```

profile of v0, /device:TPU:51, one launch (start us, length us, event | category | flops | bytes accessed | tf_op | source)
XLA Modules:
  0.0 782.9 jit_solution(3575630332409597956)
XLA Ops:
  19.0 4.6 divide_multiply_fusion
  37.0 158.8 %custom-call.4 = f32[2,16,1,64,64]{3,4,2,1,0:T(8,128)} custom-call(f32[2,16,1,64,64]{4,3,2,1,0:T(8,128)} %fusion.84), custom_call_target="InvertDiagBlocksLowerTriangular" | custom-call | tf_op jit(solution)/shard_map/vmap(jit(_solve_triangular))/vmap()/triangular_solve | solution.py:163
  195.8 3.8 fusion.55
  199.6 5.1 fusion.119
  204.8 5.3 multiply_subtract_fusion
  211.3 16.2 %while.26 = (s32[]{:T(128)}, f32[16,128,128]{2,1,0:T(8,128)}, f32[16,128,128]{2,1,0:T(8,128)}, f32[2,16,128,128]{3,2,1,0:T(8,128)}, f32[2,16,128,128]{3,2,1,0:T(8,128)}, /*index=5*/s32[]{:T(128)}, s32[]{:T(128)}) while((s32[]{:T(128)}, f32[16,128,128]{2,1,0:T(8,128)}, f32[16,128,128]{2,1,0:T(8,128)}, ...), condition=%wide.region_3.4_spmd.clone, body=%wide.region_2.3_spmd.clone.sunk | while | flops 805830656 | bytes 24118936 | solution.py:241
  215.9 3.7 convolution_add_fusion.24
  223.8 3.7 convolution_add_fusion.24
  229.1 27.0 %all_to_all.51 = f32[4,8,128,128]{3,2,1,0:T(8,128)S(1)} all-to-all(f32[4,8,128,128]{3,2,1,0:T(8,128)S(1)} %pad_maximum_fusion.1), channel_id=1, replica_groups=mesh['ctx_0'=4,'ctx_1'=4,'ctx_2'=2,'exp'=4] {'exp'}, dimensions={0} | all-to-all | bytes 4194304 | tf_op jit(solution)/shard_map/all_to_all | solution.py:34
  259.4 3.9 all-gather
  275.9 12.0 %all-gather.11.cloned.1.call-done = f32[16,128,128]{2,1,0:T(8,128)} async-done(((f32[4,128,128]{2,1,0:T(8,128)}), f32[16,128,128]{2,1,0:T(8,128)}) %all-gather.11.cloned.1.call-update) | async-done | bytes 1048592 | tf_op jit(solution)/shard_map/all_gather | solution.py:52
  293.6 20.3 %all-gather.15.cloned.1.call-done = f32[16,128,128]{2,1,0:T(8,128)} async-done(((f32[4,128,128]{2,1,0:T(8,128)}), f32[16,128,128]{2,1,0:T(8,128)}) %all-gather.15.cloned.1.call-update) | async-done | bytes 1048592 | tf_op jit(solution)/shard_map/all_gather | solution.py:52
  325.2 15.0 %all-gather.13.cloned.1.call-done = f32[16,128,128]{2,1,0:T(8,128)} async-done(((f32[4,128,128]{2,1,0:T(8,128)}), f32[16,128,128]{2,1,0:T(8,128)}) %all-gather.13.cloned.1.call-update) | async-done | bytes 1048592 | tf_op jit(solution)/shard_map/all_gather | solution.py:52
  340.2 26.1 %all-gather.17.cloned.1.call-done = f32[16,128,128]{2,1,0:T(8,128)} async-done(((f32[4,128,128]{2,1,0:T(8,128)}), f32[16,128,128]{2,1,0:T(8,128)}) %all-gather.17.cloned.1.call-update) | async-done | bytes 1048592 | tf_op jit(solution)/shard_map/all_gather | solution.py:52
  373.8 4.4 all-to-all-start.1
  388.1 11.5 %while.25 = (s32[]{:T(128)}, f32[16,128,128]{2,1,0:T(8,128)S(1)}, f32[2,16,64,128]{3,2,1,0:T(8,128)}, f32[2,16,128,128]{3,2,1,0:T(8,128)}, f32[2,16,128,128]{3,2...) while((s32[]{:T(128)}, f32[16,128,128]{2,1,0:T(8,128)S(1)}, ...), condition=%wide.region_6.7_spmd, body=%wide.region_5.6_spmd.sunk | while | flops 604372992 | bytes 17303672 | solution.py:275
  406.3 6.9 all-to-all-start.2
  418.7 14.7 %all-to-all-done.2 = bf16[4,128,2048]{2,1,0:T(8,128)(2,1)} async-done(((bf16[4,128,2048]{2,1,0:T(8,128)(2,1)}), bf16[4,128,2048]{2,1,0:T(8,128)(2,1)}, u32[]{:S(2)}, u32[]{:S(2)}) %all-to-all-start.2) | async-done | bytes 2097184 | tf_op jit(solution)/shard_map/all_to_all | solution.py:70
  433.4 3.8 fusion.59
  437.3 6.2 all-to-all-start.3
  443.8 7.5 all-to-all-done.3
  452.8 34.3 %scatter_custom_fusion = bf16[1536,2048]{1,0:T(8,128)(2,1)} fusion(s32[1280]{0:T(1024)S(1)} %broadcast_select_fusion, bf16[128,2048]{1,0:T(8,128)(2,1)S(1)} %fusion.111, s32[2048]{0:T(1024)S(1)} %pad_clamp_fusion, bf16[]{:T(256)} %constant.107.clone.1), kind=kCustom, calls=%fused_computation.28 | custom fusion | bytes 6291458
  487.1 10.8 %reshape.290 = bf16[128,2,6,2048]{3,1,0,2:T(2,128)(2,1)} reshape(bf16[256,6,2048]{2,0,1:T(8,128)(2,1)} %bitcast.344) | data formatting | bytes 12582912 | tf_op jit(solution)/shard_map/reshape | solution.py:332
  497.9 7.9 %fusion.209 = (bf16[128,2,3,2048]{3,1,0,2:T(2,128)(2,1)}, bf16[128,2,3,2048]{3,1,0,2:T(2,128)(2,1)S(1)}) fusion(bf16[128,2,6,2048]{3,1,0,2:T(2,128)(2,1)} %reshape.290), kind=kLoop, calls=%fused_computation.292 | loop fusion | bytes 12582912 | tf_op jit(solution)/shard_map/slice | solution.py:83
  505.8 3.8 copy.201
  509.6 16.2 %all-to-all-start.6 = ((bf16[128,2,3,2048]{3,1,2,0:T(2,128)(2,1)}), bf16[128,2,3,2048]{3,1,2,0:T(2,128)(2,1)}, u32[]{:S(2)}, u32[]{:S(2)}) async-start(bf16[128,2,3,2048]{3,1,2,0:T(2,128)(2,1)} %copy.201), calls=%async_computation.6 | async-start | bytes 6291456 | tf_op jit(solution)/shard_map/all_to_all | solution.py:90
  525.8 5.7 copy.197
  531.5 30.3 %all-to-all-done.6 = bf16[128,2,3,2048]{3,1,2,0:T(2,128)(2,1)} async-done(((bf16[128,2,3,2048]{3,1,2,0:T(2,128)(2,1)}), bf16[128,2,3,2048]{3,1,2,0:T(2,128)(2,1)}, u32[]{:S(2)}, u32[]{:S(2)}) %all-to-all-start.6) | async-done | bytes 3145760 | tf_op jit(solution)/shard_map/all_to_all | solution.py:90
  561.8 10.5 %all-to-all-start.4 = ((bf16[128,2,3,2048]{3,1,2,0:T(2,128)(2,1)}), bf16[128,2,3,2048]{3,1,2,0:T(2,128)(2,1)}, u32[]{:S(2)}, u32[]{:S(2)}) async-start(bf16[128,2,3,2048]{3,1,2,0:T(2,128)(2,1)} %copy.197), calls=%async_computation.4 | async-start | bytes 6291456 | tf_op jit(solution)/shard_map/all_to_all | solution.py:90
  572.3 5.2 fusion.29
  577.5 9.9 %fusion.40 = bf16[128,2,3,2048]{3,0,2,1:T(8,128)(2,1)} fusion(bf16[2,512,2048]{2,1,0:T(8,128)(2,1)} %param.35, f32[2,128,3,512]{3,1,2,0:T(8,128)S(1)} %fusion.29, bf16[2,2048,512]{2,1,0:T(8,128)(2,1)} %param.34, bf16[128,2,3,2048]{3,1,2,0:T(2,128)(2,1)} %all-to-all-done.6), kind=kOutput, calls=%fused_computation.45 | convolution fusion | flops 3225157632 | bytes 16252928 | tf_op jit(solution)/shard_map/nesf,efd->nesd/dot_general | solution.py:199
  587.4 6.8 copy.204
  594.2 13.9 %all-to-all-done.4 = bf16[128,2,3,2048]{3,1,2,0:T(2,128)(2,1)} async-done(((bf16[128,2,3,2048]{3,1,2,0:T(2,128)(2,1)}), bf16[128,2,3,2048]{3,1,2,0:T(2,128)(2,1)}, u32[]{:S(2)}, u32[]{:S(2)}) %all-to-all-start.4) | async-done | bytes 3145760 | tf_op jit(solution)/shard_map/all_to_all | solution.py:90
  608.1 10.5 %all-to-all-start.7 = ((bf16[128,2,3,2048]{3,1,2,0:T(2,128)(2,1)}), bf16[128,2,3,2048]{3,1,2,0:T(2,128)(2,1)}, u32[]{:S(2)}, u32[]{:S(2)}) async-start(bf16[128,2,3,2048]{3,1,2,0:T(2,128)(2,1)} %copy.204), calls=%async_computation.7 | async-start | bytes 6291456 | tf_op jit(solution)/shard_map/all_to_all | solution.py:329
  618.7 5.2 fusion.31
  623.8 9.9 %fusion.43 = bf16[128,2,3,2048]{3,0,2,1:T(8,128)(2,1)} fusion(bf16[2,512,2048]{2,1,0:T(8,128)(2,1)} %param.35, f32[2,128,3,512]{3,1,2,0:T(8,128)S(1)} %fusion.31, bf16[2,2048,512]{2,1,0:T(8,128)(2,1)} %param.34, bf16[128,2,3,2048]{3,1,2,0:T(2,128)(2,1)} %all-to-all-done.4), kind=kOutput, calls=%fused_computation.46 | convolution fusion | flops 3225157632 | bytes 16252928 | tf_op jit(solution)/shard_map/nesf,efd->nesd/dot_general | solution.py:199
  633.7 6.8 copy.200
  640.5 14.0 %all-to-all-done.7 = bf16[128,2,3,2048]{3,1,2,0:T(2,128)(2,1)} async-done(((bf16[128,2,3,2048]{3,1,2,0:T(2,128)(2,1)}), bf16[128,2,3,2048]{3,1,2,0:T(2,128)(2,1)}, u32[]{:S(2)}, u32[]{:S(2)}) %all-to-all-start.7) | async-done | bytes 3145760 | tf_op jit(solution)/shard_map/all_to_all | solution.py:329
  654.5 10.6 %all-to-all-start.5 = ((bf16[128,2,3,2048]{3,1,2,0:T(2,128)(2,1)}), bf16[128,2,3,2048]{3,1,2,0:T(2,128)(2,1)}, u32[]{:S(2)}, u32[]{:S(2)}) async-start(bf16[128,2,3,2048]{3,1,2,0:T(2,128)(2,1)} %copy.200), calls=%async_computation.5 | async-start | bytes 6291456 | tf_op jit(solution)/shard_map/all_to_all | solution.py:329
  665.7 10.1 %gather_fusion.1 = f32[1280]{0:T(1024)S(1)} fusion(f32[128,256]{1,0:T(8,128)S(1)} %fusion.207, s32[1280]{0:T(1024)S(1)} %reshape.312), kind=kCustom, calls=%fused_computation.2 | custom fusion | bytes 20480 | tf_op jit(solution)/shard_map/jit(take_along_axis)/gather | solution.py:298
  678.7 22.2 %all-to-all-done.5 = bf16[128,2,3,2048]{3,1,2,0:T(2,128)(2,1)} async-done(((bf16[128,2,3,2048]{3,1,2,0:T(2,128)(2,1)}), bf16[128,2,3,2048]{3,1,2,0:T(2,128)(2,1)}, u32[]{:S(2)}, u32[]{:S(2)}) %all-to-all-start.5) | async-done | bytes 3145760 | tf_op jit(solution)/shard_map/all_to_all | solution.py:329
  700.9 9.8 %pad_maximum_fusion = bf16[128,2,6,2048]{3,1,2,0:T(2,128)(2,1)S(1)} fusion(bf16[128,2,3,2048]{3,1,2,0:T(2,128)(2,1)} %all-to-all-done.7, bf16[128,2,3,2048]{3,1,2,0:T(2,128)(2,1)} %all-to-all-done.5), kind=kLoop, calls=%fused_computation.27 | loop fusion | flops 3145728 | bytes 12582912 | tf_op jit(solution)/shard_map/concatenate | solution.py:95
  710.7 6.0 copy.205
  716.7 10.1 %reshape.291 = bf16[256,6,2048]{2,0,1:T(8,128)(2,1)} reshape(bf16[128,2,6,2048]{3,1,0,2:T(2,128)(2,1)} %copy.205) | data formatting | bytes 12582912 | tf_op jit(solution)/shard_map/reshape | solution.py:340
  726.8 24.1 %gather_fusion = bf16[1280,2048]{1,0:T(8,128)(2,1)} fusion(bf16[256,6,2048]{2,0,1:T(8,128)(2,1)} %reshape.291, s32[1280]{0:T(1024)S(1)} %get-tuple-element.117), kind=kCustom, calls=%fused_computation.1 | custom fusion | bytes 10496000 | tf_op jit(solution)/shard_map/gather | solution.py:341
  750.9 10.3 %reshape.297 = f32[128,10,2048]{2,1,0:T(8,128)} reshape(bf16[1280,2048]{1,0:T(8,128)(2,1)} %gather_fusion) | data formatting | bytes 15728640 | tf_op jit(solution)/shard_map/convert_element_type | solution.py:342
  761.2 10.7 %multiply_reduce_fusion = f32[128,2048]{1,0:T(8,128)} fusion(f32[128,10,2048]{2,1,0:T(8,128)} %reshape.297, f32[128,10]{1,0:T(8,128)S(1)} %copy.208), kind=kLoop, calls=%fused_computation.26 | loop fusion | flops 4980736 | bytes 11539456 | tf_op jit(solution)/shard_map/reduce_sum | solution.py:342
  771.9 4.2 fusion.51
  (249 shorter events, 115.1 us)
Async XLA Ops:
  6.5 426.9 %copy-start = (bf16[2048,512]{1,0:T(8,128)(2,1)S(1)}, bf16[2048,512]{1,0:T(8,128)(2,1)}, u32[]{:S(2)}) copy-start(bf16[2048,512]{1,0:T(8,128)(2,1)} %param.29) | copy-start | bytes 6291460
  6.5 281.3 %all-gather.11.cloned.1.call-start = ((), (), s32[]{:S(2)}) async-start(), calls=%async_computation.8 | async-start | bytes 1310720 | tf_op jit(solution)/shard_map/all_gather | solution.py:52
  7.6 8.0 %collective-permute-start = (bf16[3,4096]{1,0:T(4,128)(2,1)S(1)}, bf16[3,4096]{1,0:T(4,128)(2,1)S(1)}, u32[]{:S(2)}, u32[]{:S(2)}) collective-permute-start(bf16[3,4096]{1,0:T(4,128)(2,1)S(1)} %slice.177), channel_id=1, source_target_pairs={{0,1},{1,2},{2,3},{3,4},{4,5},{5,6},{6,7},{7,8},{8,9},{9,10},{10,1... | collective-permute-start | bytes 73736 | tf_op jit(solution)/shard_map/ppermute | solution.py:23
  23.7 1.7 copy-start.10
  31.3 1.4 copy-start.39
  32.8 172.0 %copy-start.6 = (f32[128,8,2,128]{3,0,2,1:T(8,128)}, f32[128,8,2,128]{3,0,2,1:T(8,128)S(1)}, u32[]{:S(2)}) copy-start(f32[128,8,2,128]{3,0,2,1:T(8,128)S(1)} %broadcast_in_dim.40) | copy-start | bytes 3145732
  199.6 5.1 copy-start.8
  211.7 1.9 copy-start.2
  213.0 2.7 copy-start.4
  219.6 1.9 copy-start.2
  220.9 2.7 copy-start.4
  256.2 7.5 copy-start.12
  264.8 49.2 %all-gather.15.cloned.1.call-start = ((), (), s32[]{:S(2)}) async-start(), calls=%async_computation.10 | async-start | bytes 1310720 | tf_op jit(solution)/shard_map/all_gather | solution.py:52
  268.4 7.4 copy-start.21
  269.9 5.9 copy-start.23
  275.8 64.4 %all-gather.13.cloned.1.call-start = ((), (), s32[]{:S(2)}) async-start(), calls=%async_computation.9 | async-start | bytes 1310720 | tf_op jit(solution)/shard_map/all_gather | solution.py:52
  287.9 3.5 copy-start.5
  293.6 72.7 %all-gather.17.cloned.1.call-start = ((), (), s32[]{:S(2)}) async-start(), calls=%async_computation.11 | async-start | bytes 1310720 | tf_op jit(solution)/shard_map/all_gather | solution.py:52
  314.0 2.9 copy-start.42
  315.4 1.9 copy-start.34
  315.4 4.1 copy-start.49
  319.4 3.5 copy-start.35
  319.4 4.7 copy-start.15
  319.4 4.7 copy-start.16
  319.4 4.7 copy-start.26
  340.2 29.0 %copy-start.13 = (f32[16,128,128]{2,1,0:T(8,128)S(1)}, f32[16,128,128]{2,1,0:T(8,128)}, u32[]{:S(2)}) copy-start(f32[16,128,128]{2,1,0:T(8,128)} %all-gather.13.cloned.1.call-done) | copy-start | bytes 3145732
  366.3 2.9 copy-start.41
  370.1 1.7 copy-start.28
  370.1 1.7 copy-start.30
  373.8 14.3 %all-to-all-start.1 = ((f32[4,4,128,128]{3,2,1,0:T(8,128)}), f32[4,4,128,128]{3,2,1,0:T(8,128)S(1)}, u32[]{:S(2)}, u32[]{:S(2)}) async-start(f32[4,4,128,128]{3,2,1,0:T(8,128)} %pad_maximum_fusion.2), calls=%async_computation.1 | async-start | bytes 2097152 | tf_op jit(solution)/shard_map/all_to_all | solution.py:263
  378.2 1.4 copy-start.7
  378.2 3.2 copy-start.9
  388.1 3.2 copy-start.3
  393.9 3.2 copy-start.3
  399.7 3.9 copy-start.45
  406.3 6.9 copy-start.46
  406.3 27.1 %all-to-all-start.2 = ((bf16[4,128,2048]{2,1,0:T(8,128)(2,1)}), bf16[4,128,2048]{2,1,0:T(8,128)(2,1)}, u32[]{:S(2)}, u32[]{:S(2)}) async-start(bf16[4,128,2048]{2,1,0:T(8,128)(2,1)} %broadcast_in_dim.46), calls=%async_computation.2 | async-start | bytes 4194304 | tf_op jit(solution)/shard_map/all_to_all | solution.py:70
  414.2 1.4 copy-start.11
  437.3 6.3 copy-start.51
  437.3 6.4 copy-start.50
  437.3 14.0 %all-to-all-start.3 = ((f32[4,128,512]{2,1,0:T(8,128)}), f32[4,128,512]{2,1,0:T(8,128)S(1)}, u32[]{:S(2)}, u32[]{:S(2)}) async-start(f32[4,128,512]{2,1,0:T(8,128)} %fusion.59), calls=%async_computation.3 | async-start | bytes 2097152 | tf_op jit(solution)/shard_map/all_to_all | solution.py:289
  509.6 52.2 %all-to-all-start.6 = ((bf16[128,2,3,2048]{3,1,2,0:T(2,128)(2,1)}), bf16[128,2,3,2048]{3,1,2,0:T(2,128)(2,1)}, u32[]{:S(2)}, u32[]{:S(2)}) async-start(bf16[128,2,3,2048]{3,1,2,0:T(2,128)(2,1)} %copy.201), calls=%async_computation.6 | async-start | bytes 6291456 | tf_op jit(solution)/shard_map/all_to_all | solution.py:90
  561.8 46.3 %all-to-all-start.4 = ((bf16[128,2,3,2048]{3,1,2,0:T(2,128)(2,1)}), bf16[128,2,3,2048]{3,1,2,0:T(2,128)(2,1)}, u32[]{:S(2)}, u32[]{:S(2)}) async-start(bf16[128,2,3,2048]{3,1,2,0:T(2,128)(2,1)} %copy.197), calls=%async_computation.4 | async-start | bytes 6291456 | tf_op jit(solution)/shard_map/all_to_all | solution.py:90
  608.1 46.4 %all-to-all-start.7 = ((bf16[128,2,3,2048]{3,1,2,0:T(2,128)(2,1)}), bf16[128,2,3,2048]{3,1,2,0:T(2,128)(2,1)}, u32[]{:S(2)}, u32[]{:S(2)}) async-start(bf16[128,2,3,2048]{3,1,2,0:T(2,128)(2,1)} %copy.204), calls=%async_computation.7 | async-start | bytes 6291456 | tf_op jit(solution)/shard_map/all_to_all | solution.py:329
  640.5 24.8 %copy-start.48 = (bf16[2048]{0:T(1024)(128)(2,1)S(1)}, bf16[2048]{0:T(1024)(128)(2,1)}, u32[]{:S(2)}) copy-start(bf16[2048]{0:T(1024)(128)(2,1)} %param.39) | copy-start | bytes 12292
  640.5 24.8 %copy-start.52 = (bf16[2048,256]{1,0:T(8,128)(2,1)S(1)}, bf16[2048,256]{1,0:T(8,128)(2,1)}, u32[]{:S(2)}) copy-start(bf16[2048,256]{1,0:T(8,128)(2,1)} %param.31) | copy-start | bytes 3145732
  654.5 46.4 %all-to-all-start.5 = ((bf16[128,2,3,2048]{3,1,2,0:T(2,128)(2,1)}), bf16[128,2,3,2048]{3,1,2,0:T(2,128)(2,1)}, u32[]{:S(2)}, u32[]{:S(2)}) async-start(bf16[128,2,3,2048]{3,1,2,0:T(2,128)(2,1)} %copy.200), calls=%async_computation.5 | async-start | bytes 6291456 | tf_op jit(solution)/shard_map/all_to_all | solution.py:329
  761.2 14.9 %copy-start.1 = (bf16[2048,512]{1,0:T(8,128)(2,1)S(1)}, bf16[2048,512]{1,0:T(8,128)(2,1)}, u32[]{:S(2)}) copy-start(bf16[2048,512]{1,0:T(8,128)(2,1)} %param.29) | copy-start | bytes 6291460
  (20 other events, 20.1 us)
Sparse Core Ops, SparseCore 0:
  264.9 22.9 all-gather.10
  289.5 24.4 all-gather.14
  315.6 24.5 all-gather.12
  341.7 24.5 all-gather.16
where the time goes:
time: 797 us; the launch traced here: 783 us
  other arithmetic  201 us (25%)
  waiting for transfers between devices  178 us (22%)
  local copies, waits for them, and re-layouts  172 us (22%)
  matrix products  116 us (15%)
  starting transfers between devices  68.4 us (9%)
  blocking collectives  33.1 us (4%)
  between operations  14.5 us (2%)
    another operation x4, other arithmetic, span_terms(): jax.scipy.linalg.solve_triangular(system, right_operand, lower=True, unit...  159 us
    all_gather x4, waiting for transfers between devices, entering(): pieces = jax.tree.map(lambda part: lax.all_gather(part, axis), subtotal)  73.4 us
    dot_general x39, matrix products, apply_map(): jnp.einsum('coq,cqd->cod', left_transform, right_operand, precision=highe...  45.2 us
    all_to_all x2, waiting for transfers between devices, grouped_exchange(): lax.all_to_all(group, axis, split_axis=split_dim, concat_axis=concat_dim,...  44.2 us
    unnamed x104, local copies, waits for them, and re-layouts  44 us
    all_to_all x2, waiting for transfers between devices, serve_slots(): lax.all_to_all(result, CTX_EXP, split_axis=0, concat_axis=0, tiled=True)  36.2 us
    all_to_all x1, blocking collectives, sent_together(): lax.all_to_all(both, axis, split_axis=split_dim, concat_axis=concat_dim,...  27 us
    all_to_all x2, starting transfers between devices, grouped_exchange(): lax.all_to_all(group, axis, split_axis=split_dim, concat_axis=concat_dim,...  26.7 us
  transfers between devices with their start and end apart: 12, of which 11 were waited for; matrix products, arithmetic and copies ran while one was open for 13% of the time, Pallas kernels for 0%

commit v1 on v0

v1 whole, which is shorter than its diff:
```python
import jax
import jax.numpy as jnp
import numpy as np
from jax import lax
from jax.experimental import pallas as pl
from jax.experimental.pallas import tpu as pltpu
from jax.sharding import Mesh
from jax.sharding import PartitionSpec as P

VHEADS = 16
HEAD = 128
ROWS = 128
TOP = 10
CAP = 6
WIDTH = 2048
EXPERTS = 256
AXES = ("ctx_0", "ctx_1", "ctx_2", "exp")
SAME_CORE = ("ctx_0", "ctx_1", "exp")
PEERS = 64
SLOTS = 4 * CAP
SENT = PEERS * SLOTS
BATCH = 8
MESH = pl.DeviceIdType.MESH
epsilon = 1e-06
F32 = jnp.float32
BF16 = jnp.bfloat16
VM = pl.BlockSpec(memory_space=pltpu.VMEM)
ANY = pl.BlockSpec(memory_space=pl.ANY)


def nn(a, b):
    return lax.dot_general(a, b, (((1,), (0,)), ((), ())), preferred_element_type=F32)


def nt(a, b):
    return lax.dot_general(a, b, (((1,), (1,)), ((), ())), preferred_element_type=F32)


def tn(a, b):
    return lax.dot_general(a, b, (((0,), (0,)), ((), ())), preferred_element_type=F32)


def silu(v):
    return v / (1.0 + jnp.exp(-v))


def local_kernel(
    q_ref, k_ref, v_ref, qb_ref, kb_ref, vb_ref, qw_ref, kw_ref, vw_ref, ld_ref, ws_ref,
    maps_ref, reads_ref, offs_ref, pad, cumt, lows, inv,
):
    first = pl.program_id(0) * BATCH
    rows = lax.broadcasted_iota(jnp.int32, (ROWS, ROWS), 0)
    cols = lax.broadcasted_iota(jnp.int32, (ROWS, ROWS), 1)
    causal = rows >= cols
    strict = rows > cols
    ones = causal.astype(F32)
    decay = ld_ref[...]
    highest = lax.Precision.HIGHEST
    cum = lax.dot_general(
        ones, decay, (((1,), (0,)), ((), ())), precision=highest, preferred_element_type=F32
    )
    cumt[...] = lax.dot_general(
        decay, ones, (((0,), (1,)), ((), ())), precision=highest, preferred_element_type=F32
    )
    strength = ws_ref[...]
    lane = lax.broadcasted_iota(jnp.int32, (ROWS, VHEADS), 1)

    def column(table, head):
        return jnp.sum(jnp.where(lane == head, table, 0.0), axis=1, keepdims=True)

    def activated(x_ref, b_ref, w_ref):
        n = x_ref.shape[1]
        pad[0:8, 0:n] = b_ref[...].astype(F32)
        pad[8 : 8 + ROWS, 0:n] = x_ref[...].astype(F32)
        total = w_ref[3:4, :] * pad[8 : 8 + ROWS, 0:n]
        for tap in range(3):
            total = total + w_ref[tap : tap + 1, :] * pad[5 + tap : 5 + tap + ROWS, 0:n]
        return silu(total)

    def unit(a):
        return a * lax.rsqrt(jnp.sum(a * a, axis=-1, keepdims=True) + epsilon)

    queries = activated(q_ref, qb_ref, qw_ref)
    keys = activated(k_ref, kb_ref, kw_ref)
    values = activated(v_ref, vb_ref, vw_ref)
    eye = (rows == cols).astype(F32)
    per_head = []
    for pair in range(BATCH // 2):
        part = slice(pair * HEAD, (pair + 1) * HEAD)
        query = unit(queries[:, part]) * HEAD ** (-0.5)
        key = unit(keys[:, part])
        key_b = key.astype(BF16)
        inner = nt(key_b, key_b)
        scores = nt(query.astype(BF16), key_b)
        for i in (2 * pair, 2 * pair + 1):
            c = column(cum, first + i)
            b = column(strength, first + i)
            gap = c - cumt[pl.ds(first + i, 1), :]
            ratios = jnp.where(causal, jnp.exp(jnp.where(causal, gap, 0.0)), 0.0)
            low = jnp.where(strict, ratios * inner, 0.0) * b
            lows[i] = low
            inv[i] = eye - jnp.where((rows >> 1) == (cols >> 1), low, 0.0)
            last = c[ROWS - 1 : ROWS, :]
            decays = jnp.exp(c)
            right = jnp.concatenate(
                [(b * decays * key).astype(BF16), (b * values[:, i * HEAD : (i + 1) * HEAD]).astype(BF16)],
                axis=1,
            )
            per_head.append(
                (
                    (scores * ratios).astype(BF16),
                    query * decays,
                    (key * jnp.exp(last - c)).astype(BF16),
                    right,
                    jnp.exp(last) - 1.0,
                )
            )
    for level in range(1, 7):
        here = ((rows >> (level + 1)) == (cols >> (level + 1))) & ((rows >> level) != (cols >> level))
        for i in range(BATCH):
            x = inv[i]
            x_b = x.astype(BF16)
            off = jnp.where(here, lows[i], 0.0).astype(BF16)
            inv[i] = x - nn(x_b, nn(off, x_b).astype(BF16))
    for i in range(BATCH):
        score, read, end_key, right, less = per_head[i]
        solved = nn(inv[i].astype(BF16), right).astype(BF16)
        carried = tn(solved, end_key)
        maps_ref[i, 0:HEAD, :] = (less * eye - carried[0:HEAD]).astype(BF16)
        maps_ref[i, HEAD : 2 * HEAD, :] = carried[HEAD:].astype(BF16)
        produced = nn(score, solved)
        reads_ref[i] = (read - produced[:, 0:HEAD]).astype(BF16)
        offs_ref[i] = produced[:, HEAD:]


def local_terms(mixed, before, conv_weight, log_decay, write_strength):
    n = BATCH // 2 * HEAD
    steps = VHEADS // BATCH

    def wide(rows_of, width, base):
        return pl.BlockSpec((rows_of, width), lambda s: (0, base + s))

    def three(rows_of):
        return [wide(rows_of, n, 0), wide(rows_of, n, steps), wide(rows_of, 2 * n, steps)]

    whole = pl.BlockSpec((ROWS, VHEADS), lambda s: (0, 0))
    return pl.pallas_call(
        local_kernel,
        name="local_terms",
        grid=(steps,),
        in_specs=three(ROWS) + three(8) + three(4) + [whole, whole],
        out_specs=[
            pl.BlockSpec((BATCH, 2 * HEAD, HEAD), lambda s: (s, 0, 0)),
            pl.BlockSpec((BATCH, ROWS, HEAD), lambda s: (s, 0, 0)),
            pl.BlockSpec((BATCH, ROWS, HEAD), lambda s: (s, 0, 0)),
        ],
        out_shape=[
            jax.ShapeDtypeStruct((VHEADS, 2 * HEAD, HEAD), BF16),
            jax.ShapeDtypeStruct((VHEADS, ROWS, HEAD), BF16),
            jax.ShapeDtypeStruct((VHEADS, ROWS, HEAD), F32),
        ],
        scratch_shapes=[
            pltpu.VMEM((8 + ROWS, 2 * n), F32),
            pltpu.VMEM((VHEADS, ROWS), F32),
            pltpu.VMEM((BATCH, ROWS, ROWS), F32),
            pltpu.VMEM((BATCH, ROWS, ROWS), F32),
        ],
        compiler_params=pltpu.CompilerParams(vmem_limit_bytes=40 << 20),
        cost_estimate=pl.CostEstimate(
            flops=8_000_000_000, bytes_accessed=6_000_000, transcendentals=1_000_000
        ),
    )(
        mixed, mixed, mixed, before, before, before, conv_weight, conv_weight, conv_weight,
        log_decay, write_strength,
    )


def scan_kernel(
    maps, starts, got1, pre1, tot1, got2, pre2, tot2, got3, st4, got4, st5, got5,
    send1, recv1, send2, recv2, send3, recv3, send4, recv4, send5, recv5,
):
    z, x, c, y = (lax.axis_index(a) for a in AXES)
    place = 2 * x + c
    barrier = pltpu.get_barrier_semaphore()

    def at(j, axis):
        if axis == "y":
            return {"exp": lax.rem(y + j, 4)}
        if axis == "z":
            return {"ctx_0": lax.rem(z + j, 4)}
        other = lax.rem(place + j, 8)
        return {"ctx_1": other // 2, "ctx_2": lax.rem(other, 2)}

    for axis, count in (("y", 4), ("z", 4), ("p", 8)):
        for j in range(1, count):
            pl.semaphore_signal(barrier, inc=1, device_id=at(j, axis), device_id_type=MESH)
    pl.semaphore_wait(barrier, 13)
    started = []

    def send(src, dst, s, r, device):
        copy = pltpu.make_async_remote_copy(
            src_ref=src, dst_ref=dst, send_sem=s, recv_sem=r, device_id=device, device_id_type=MESH
        )
        copy.start()
        started.append(copy)
        return copy

    copies = []
    for j in range(1, 4):
        other = lax.rem(y + j, 4)
        copies.append(
            send(maps.at[pl.ds(4 * other, 4)], got1.at[y], send1.at[j], recv1.at[j], at(j, "y"))
        )
    got1[y] = maps[pl.ds(4 * y, 4)]
    for copy in copies:
        copy.wait_recv()
    for h in range(4):
        run = got1[0, h].astype(F32)
        for m in range(1, 4):
            pre1[m - 1, h] = run.astype(BF16)
            run = run + got1[m, h].astype(F32) + nn(run.astype(BF16), got1[m, h, 0:HEAD, :])
        tot1[h] = run.astype(BF16)

    copies = []
    for j in range(1, 8):
        other = lax.rem(place + j, 8)
        head, half = other // 2, lax.rem(other, 2)
        copies.append(
            send(
                tot1.at[head, 0:HEAD], got2.at[place, 0:HEAD], send2.at[j, 0], recv2.at[j, 0],
                at(j, "p"),
            )
        )
        copies.append(
            send(
                tot1.at[head, pl.ds(pl.multiple_of(HEAD + 64 * half, 64), 64)],
                got2.at[place, HEAD : HEAD + 64],
                send2.at[j, 1], recv2.at[j, 1], at(j, "p"),
            )
        )
    got2[place, 0:HEAD, :] = tot1[x, 0:HEAD, :]
    got2[place, HEAD : HEAD + 64, :] = tot1[x, pl.ds(pl.multiple_of(HEAD + 64 * c, 64), 64), :]
    for copy in copies:
        copy.wait_recv()
    run = got2[0].astype(F32)
    for p in range(1, 8):
        pre2[p - 1] = run.astype(BF16)
        run = run + got2[p].astype(F32) + nn(run.astype(BF16), got2[p, 0:HEAD, :])
    tot2[...] = run.astype(BF16)

    copies = []
    for j in range(1, 4):
        copies.append(send(tot2, got3.at[z], send3.at[j], recv3.at[j], at(j, "z")))
    got3[z] = tot2[...]
    for copy in copies:
        copy.wait_recv()
    state = jnp.zeros((64, HEAD), F32)
    for k in range(3):
        later = state + got3[k, HEAD:, :].astype(F32) + nn(state.astype(BF16), got3[k, 0:HEAD, :])
        state = jnp.where(k < z, later, state)
    state_b = state.astype(BF16)
    st4[0] = state_b
    for p in range(1, 8):
        st4[p] = (
            state + pre2[p - 1, HEAD:, :].astype(F32) + nn(state_b, pre2[p - 1, 0:HEAD, :])
        ).astype(BF16)

    copies = []
    rows_here = pl.ds(pl.multiple_of(64 * c, 64), 64)
    for j in range(1, 8):
        other = lax.rem(place + j, 8)
        copies.append(
            send(st4.at[other], got4.at[x, rows_here], send4.at[j], recv4.at[j], at(j, "p"))
        )
    got4[x, rows_here, :] = st4[place]
    for copy in copies:
        copy.wait_recv()
    for h in range(4):
        begin = got4[h]
        st5[0, h] = begin
        for m in range(1, 4):
            st5[m, h] = (
                begin.astype(F32)
                + pre1[m - 1, h, HEAD:, :].astype(F32)
                + nn(begin, pre1[m - 1, h, 0:HEAD, :])
            ).astype(BF16)

    copies = []
    for j in range(1, 4):
        other = lax.rem(y + j, 4)
        copies.append(send(st5.at[other], got5.at[y], send5.at[j], recv5.at[j], at(j, "y")))
    got5[y] = st5[y]
    for copy in copies:
        copy.wait_recv()
    for m in range(4):
        starts[4 * m : 4 * m + 4] = got5[m]
    for copy in started:
        copy.wait_send()


def scan_states(maps):
    dma = pltpu.SemaphoreType.DMA
    return pl.pallas_call(
        scan_kernel,
        name="scan_states",
        in_specs=[VM],
        out_specs=VM,
        out_shape=jax.ShapeDtypeStruct((VHEADS, HEAD, HEAD), BF16),
        scratch_shapes=[
            pltpu.VMEM((4, 4, 2 * HEAD, HEAD), BF16),
            pltpu.VMEM((3, 4, 2 * HEAD, HEAD), BF16),
            pltpu.VMEM((4, 2 * HEAD, HEAD), BF16),
            pltpu.VMEM((8, HEAD + 64, HEAD), BF16),
            pltpu.VMEM((7, HEAD + 64, HEAD), BF16),
            pltpu.VMEM((HEAD + 64, HEAD), BF16),
            pltpu.VMEM((4, HEAD + 64, HEAD), BF16),
            pltpu.VMEM((8, 64, HEAD), BF16),
            pltpu.VMEM((4, HEAD, HEAD), BF16),
            pltpu.VMEM((4, 4, HEAD, HEAD), BF16),
            pltpu.VMEM((4, 4, HEAD, HEAD), BF16),
            dma((4,)), dma((4,)), dma((8, 2)), dma((8, 2)), dma((4,)), dma((4,)),
            dma((8,)), dma((8,)), dma((4,)), dma((4,)),
        ],
        compiler_params=pltpu.CompilerParams(
            collective_id=0, has_side_effects=True, vmem_limit_bytes=32 << 20
        ),
        cost_estimate=pl.CostEstimate(
            flops=30_000_000_000, bytes_accessed=4_000_000, transcendentals=0
        ),
    )(maps)


def mix_kernel(
    reads, offs, starts, gate_ref, gain_ref, res_ref, post_ref, own, a1, a2, a3, b1, b2, b3,
    after_ref, routed_ref, weights, normed, total, sems,
):
    c, y = lax.axis_index("ctx_2"), lax.axis_index("exp")
    half = WIDTH // 2
    mine = pl.ds(pl.multiple_of(half * c, half), half)
    theirs = pl.ds(pl.multiple_of(half * (1 - c), half), half)
    loads = [[pltpu.make_async_copy(own, weights.at[0], sems.at[0])]]
    for j, (a, b) in enumerate(((a1, b1), (a2, b2), (a3, b3)), 1):
        loads.append(
            [
                pltpu.make_async_copy(a, weights.at[j, mine], sems.at[2 * j - 1]),
                pltpu.make_async_copy(b, weights.at[j, theirs], sems.at[2 * j]),
            ]
        )
    for group in loads:
        for load in group:
            load.start()
    gain = gain_ref[...]
    for h in range(VHEADS):
        part = slice(h * HEAD, (h + 1) * HEAD)
        out = offs[h] + nt(reads[h], starts[h])
        out = out * lax.rsqrt(jnp.mean(out * out, axis=-1, keepdims=True) + epsilon)
        normed[:, part] = (out * gain * silu(gate_ref[:, part].astype(F32))).astype(BF16)
    columns = WIDTH // 4
    for j in range(4):
        for load in loads[j]:
            load.wait()
        block = lax.rem(y + 4 - j, 4)
        here = pl.ds(pl.multiple_of(columns * block, columns), columns)
        total[:, here] = nn(normed[...], weights[j])
    after = (res_ref[...].astype(F32) + total[...]).astype(BF16)
    after_ref[...] = after
    wide = after.astype(F32)
    routed_ref[...] = (
        wide * lax.rsqrt(jnp.mean(wide * wide, axis=-1, keepdims=True) + epsilon) * post_ref[...]
    ).astype(BF16)


def mix(reads, offs, starts, gate, gain, residual, post, own, near, far):
    shape = jax.ShapeDtypeStruct((ROWS, WIDTH), BF16)
    return pl.pallas_call(
        mix_kernel,
        name="mix",
        in_specs=[VM] * 7 + [ANY] * 7,
        out_specs=[VM, VM],
        out_shape=[shape, shape],
        scratch_shapes=[
            pltpu.VMEM((4, WIDTH, WIDTH // 4), BF16),
            pltpu.VMEM((ROWS, WIDTH), BF16),
            pltpu.VMEM((ROWS, WIDTH), F32),
            pltpu.SemaphoreType.DMA((7,)),
        ],
        compiler_params=pltpu.CompilerParams(vmem_limit_bytes=40 << 20),
        cost_estimate=pl.CostEstimate(
            flops=2_000_000_000, bytes_accessed=12_000_000, transcendentals=300_000
        ),
    )(reads, offs, starts, gate, gain, residual, post, own, *near, *far)


LANES = np.arange(SENT)
PEER, INSIDE = LANES // SLOTS, LANES % SLOTS
EXPERT_OF = 2 * (PEER // 4 * 8 + PEER % 4) + INSIDE // (2 * CAP)
TABLE = np.stack(
    [EXPERT_OF, INSIDE % (2 * CAP) // CAP, INSIDE % CAP] + [np.zeros(SENT, np.int64)] * 5
).astype(np.int32)


def slot_kernel(ids_ref, table_ref, sel_ref):
    c = lax.axis_index("ctx_2")
    wanted = table_ref[0:1, :] + 8 * c
    source, slot = table_ref[1:2, :], table_ref[2:3, :]
    rows = lax.broadcasted_iota(jnp.int32, (ROWS, ROWS), 0)
    cols = lax.broadcasted_iota(jnp.int32, (ROWS, ROWS), 1)
    earlier = (rows > cols).astype(BF16)
    for half in range(2):
        part = slice(half * ROWS, (half + 1) * ROWS)
        ids = ids_ref[part, :]
        hit = (ids[:, 0:1] == wanted) & (source == half)
        for k in range(1, TOP):
            hit = hit | ((ids[:, k : k + 1] == wanted) & (source == half))
        marks = hit.astype(F32)
        rank = nn(earlier, marks.astype(BF16))
        sel_ref[part, :] = jnp.where(rank == slot.astype(F32), marks, 0.0).astype(BF16)


def slots(ids):
    return pl.pallas_call(
        slot_kernel,
        name="slots",
        in_specs=[VM, VM],
        out_specs=VM,
        out_shape=jax.ShapeDtypeStruct((2 * ROWS, SENT), BF16),
        compiler_params=pltpu.CompilerParams(vmem_limit_bytes=32 << 20),
        cost_estimate=pl.CostEstimate(
            flops=200_000_000, bytes_accessed=1_000_000, transcendentals=0
        ),
    )(ids, jnp.asarray(TABLE))


def send_kernel(own, other, sel_ref, ids_ref, table_ref, router, out_ref, high_ref, low_ref):
    rows = jnp.concatenate([own[...], other[...]], axis=0)

    @pl.when(pl.program_id(0) == 0)
    def _():
        logits = nn(rows, router[...])
        lane = lax.broadcasted_iota(jnp.int32, (2 * ROWS, EXPERTS), 1)
        ids = ids_ref[...]
        hit = ids[:, 0:1] == lane
        for k in range(1, TOP):
            hit = hit | (ids[:, k : k + 1] == lane)
        chosen = jnp.where(hit, jnp.exp(jnp.where(hit, logits, 0.0)), 0.0)
        gates = chosen / jnp.sum(chosen, axis=1, keepdims=True)
        wanted = table_ref[0:1, :] + 8 * lax.axis_index("ctx_2")
        spread = (
            lax.broadcasted_iota(jnp.int32, (EXPERTS, SENT), 0) == wanted
        ).astype(BF16)
        high = gates.astype(BF16)
        low = (gates - high.astype(F32)).astype(BF16)
        sel = sel_ref[...]
        high_ref[...] = nn(high, spread).astype(BF16) * sel
        low_ref[...] = nn(low, spread).astype(BF16) * sel

    n = out_ref.shape[1]
    here = pl.ds(pl.multiple_of(pl.program_id(0) * n, n), n)
    cut = jnp.concatenate([own[:, here], other[:, here]], axis=0)
    out_ref[...] = tn(sel_ref[...], cut).astype(BF16)


def to_send(own, other, sel, ids, router):
    n = 256
    full = lambda *shape: pl.BlockSpec(shape, lambda s: (0,) * len(shape))
    return pl.pallas_call(
        send_kernel,
        name="to_send",
        grid=(WIDTH // n,),
        in_specs=[
            full(ROWS, WIDTH), full(ROWS, WIDTH), full(2 * ROWS, SENT), full(2 * ROWS, TOP),
            full(8, SENT), full(WIDTH, EXPERTS),
        ],
        out_specs=[
            pl.BlockSpec((SENT, n), lambda s: (0, s)), full(2 * ROWS, SENT), full(2 * ROWS, SENT),
        ],
        out_shape=[
            jax.ShapeDtypeStruct((SENT, WIDTH), BF16),
            jax.ShapeDtypeStruct((2 * ROWS, SENT), BF16),
            jax.ShapeDtypeStruct((2 * ROWS, SENT), BF16),
        ],
        compiler_params=pltpu.CompilerParams(vmem_limit_bytes=40 << 20),
        cost_estimate=pl.CostEstimate(
            flops=2_000_000_000, bytes_accessed=10_000_000, transcendentals=70_000
        ),
    )(own, other, sel, ids, jnp.asarray(TABLE), router)


def expert_kernel(x_ref, gate_ref, up_ref, down_ref, out_ref):
    x = x_ref[...]
    n = x.shape[0]
    inside = lax.rem(lax.broadcasted_iota(jnp.int32, (n, 1), 0), SLOTS)
    total = None
    for e in range(2):
        hidden = silu(nn(x, gate_ref[e])) * nn(x, up_ref[e])
        hidden = jnp.where((inside >= 2 * CAP) == bool(e), hidden, 0.0).astype(BF16)
        part = nn(hidden, down_ref[e])
        total = part if total is None else total + part
    out_ref[...] = total.astype(BF16)


def run_experts(received, gate, up, down):
    n = SENT // 8
    once = lambda a: pl.BlockSpec(a.shape, lambda s: (0, 0, 0), pipeline_mode=pl.Buffered(1))
    rows = pl.BlockSpec((n, WIDTH), lambda s: (s, 0))
    return pl.pallas_call(
        expert_kernel,
        name="experts",
        grid=(SENT // n,),
        in_specs=[rows, once(gate), once(up), once(down)],
        out_specs=rows,
        out_shape=jax.ShapeDtypeStruct((SENT, WIDTH), BF16),
        compiler_params=pltpu.CompilerParams(vmem_limit_bytes=48 << 20),
        cost_estimate=pl.CostEstimate(
            flops=20_000_000_000, bytes_accessed=24_000_000, transcendentals=1_600_000
        ),
    )(received, gate, up, down)


def exchange(x):
    return lax.all_to_all(x, SAME_CORE, split_axis=0, concat_axis=0, tiled=True)


def gather_kernel(back, high_ref, low_ref, mine_ref, theirs_ref):
    rows = back[...]
    both = nn(high_ref[...], rows) + nn(low_ref[...], rows)
    mine_ref[...] = both[0:ROWS]
    theirs_ref[...] = both[ROWS:]


def gathered(back, high, low):
    n = 256
    full = lambda *shape: pl.BlockSpec(shape, lambda s: (0,) * len(shape))
    part = pl.BlockSpec((ROWS, n), lambda s: (0, s))
    shape = jax.ShapeDtypeStruct((ROWS, WIDTH), F32)
    return pl.pallas_call(
        gather_kernel,
        name="gathered",
        grid=(WIDTH // n,),
        in_specs=[
            pl.BlockSpec((SENT, n), lambda s: (0, s)), full(2 * ROWS, SENT), full(2 * ROWS, SENT),
        ],
        out_specs=[part, part],
        out_shape=[shape, shape],
        compiler_params=pltpu.CompilerParams(vmem_limit_bytes=32 << 20),
        cost_estimate=pl.CostEstimate(
            flops=3_000_000_000, bytes_accessed=9_000_000, transcendentals=0
        ),
    )(back, high, low)


def from_other_core(a):
    return lax.ppermute(a, "ctx_2", [(0, 1), (1, 0)])


def local(
    residual, mixed_qkv, output_gate, log_decay, write_strength, conv_weight, norm_gain,
    out_weight, post_gain, router_weight, expert_ids, expert_gate, expert_up, expert_down,
    shared_gate, shared_up, shared_down, shared_switch,
):
    count = 128
    before = lax.ppermute(
        mixed_qkv[ROWS - 8 :], AXES, [(k, k + 1) for k in range(count - 1)]
    )
    half = WIDTH // 2
    own_half = lax.dynamic_slice_in_dim(out_weight, lax.axis_index("ctx_2") * half, half, 0)
    near = [
        lax.ppermute(own_half, "exp", [(k, (k + j) % 4) for k in range(4)]) for j in (1, 2, 3)
    ]
    far = [from_other_core(a) for a in near]
    maps, reads, offs = local_terms(mixed_qkv, before, conv_weight, log_decay, write_strength)
    starts = scan_states(maps)
    ids = jnp.concatenate([expert_ids, from_other_core(expert_ids)], axis=0)
    sel = slots(ids)
    after_mix, routed_in = mix(
        reads, offs, starts, output_gate, norm_gain.reshape(1, HEAD), residual,
        post_gain.reshape(1, WIDTH), out_weight, near, far,
    )
    outgoing, high, low = to_send(routed_in, from_other_core(routed_in), sel, ids, router_weight)
    received = exchange(outgoing.reshape(PEERS, SLOTS, WIDTH)).reshape(SENT, WIDTH)
    result = run_experts(received, expert_gate, expert_up, expert_down)
    returned = exchange(result.reshape(PEERS, SLOTS, WIDTH)).reshape(SENT, WIDTH)
    mine, theirs = gathered(returned, high, low)
    shared_hidden = (
        jax.nn.silu(jnp.dot(routed_in, shared_gate, preferred_element_type=F32))
        * jnp.dot(routed_in, shared_up, preferred_element_type=F32)
    ).astype(BF16)
    switch_rows = jax.nn.sigmoid(jnp.dot(routed_in, shared_switch, preferred_element_type=F32))
    shared_out = switch_rows[:, None] * jnp.dot(
        shared_hidden, shared_down, preferred_element_type=F32
    )
    return (after_mix.astype(F32) + shared_out + mine + from_other_core(theirs)).astype(BF16)


def solution(mesh):
    finer = Mesh(mesh.devices.reshape(4, 4, 2, mesh.shape["exp"]), AXES)
    rows = P(AXES, None)
    held = P(AXES, None, None)
    placed = (
        rows, rows, rows, rows, rows, P(), P(), P(None, "exp"), P(), P(), rows, held, held, held,
        P(), P(), P(), P(),
    )
    return jax.shard_map(local, mesh=finer, in_specs=placed, out_specs=rows, check_vma=False)
```

time: 797 us -> 335 us (0.42); the launches traced: 783 us -> 331 us
  other arithmetic: 201 us -> 0.01 us
  local copies, waits for them, and re-layouts: 172 us -> 9.26 us
  waiting for transfers between devices: 178 us -> 44.2 us
  blocking collectives: 33.1 us -> 162 us
  matrix products: 116 us -> 4.64 us
  Pallas kernels: 0 us -> 98.4 us
  starting transfers between devices: 68.4 us -> 11.4 us
  between operations: 14.5 us -> 0.26 us
    another operation x9 -> x0, other arithmetic: 163 us -> none  [the longest x4 159 us: span_terms(): jax.scipy.linalg.solve_triangular(system, right_operand, lower=True, unit...]
    all_to_all x1 -> x2, blocking collectives: 27 us -> 162 us  [exchange(): return lax.all_to_all(x, SAME_CORE, split_axis=0, concat_axis=0, tiled=True)]
    dot_general x56 -> x3, matrix products: 112 us -> 4.64 us  [the longest x1 3.93 us: local(): jnp.dot(shared_hidden, shared_down, preferred_element_type=F32)]
    all_to_all x7 -> x0, waiting for transfers between devices: 105 us -> none  [the longest x2 44.2 us: grouped_exchange(): lax.all_to_all(group, axis, split_axis=split_dim, concat_axis=concat_dim,...]
    pallas_call x0 -> x7, Pallas kernels: none -> 98.4 us  [the longest x1 41.5 us: scan_states(): pl.pallas_call(scan_kernel, name='scan_states', in_specs=[VM], out_specs=...]
    all_gather x4 -> x0, waiting for transfers between devices: 73.4 us -> none  [entering(): pieces = jax.tree.map(lambda part: lax.all_gather(part, axis), subtotal)]
    all_to_all x7 -> x0, starting transfers between devices: 65.3 us -> none  [the longest x2 26.7 us: grouped_exchange(): lax.all_to_all(group, axis, split_axis=split_dim, concat_axis=concat_dim,...]
    ppermute x1 -> x10, waiting for transfers between devices: 0.01 us -> 44.2 us  [the longest x1 41.2 us: local(): lax.ppermute(mixed_qkv[ROWS - 8:], AXES, [(k, k + 1) for k in range(count...]
  transfers between devices with their start and end apart: 12 -> 10, of which waited for: 11 -> 3; matrix products, arithmetic and copies ran while one was open for 13% -> 1% of each run, Pallas kernels for 0% -> 17%
where the time goes in v1:
time: 335 us; the launch traced here: 331 us
  blocking collectives  162 us (48%)
  Pallas kernels  98.4 us (29%)
  waiting for transfers between devices  44.2 us (13%)
  starting transfers between devices  11.4 us (3%)
  local copies, waits for them, and re-layouts  9.26 us (3%)
  matrix products  4.64 us (1%)
    all_to_all x2, blocking collectives, exchange(): return lax.all_to_all(x, SAME_CORE, split_axis=0, concat_axis=0, tiled=True)  162 us
    pallas_call x1, Pallas kernels, scan_states(): pl.pallas_call(scan_kernel, name='scan_states', in_specs=[VM], out_specs=...  41.5 us
    ppermute x1, waiting for transfers between devices, local(): lax.ppermute(mixed_qkv[ROWS - 8:], AXES, [(k, k + 1) for k in range(count...  41.2 us
    pallas_call x1, Pallas kernels, run_experts(): pl.pallas_call(expert_kernel, name='experts', grid=(SENT // n,), in_specs...  26.6 us
    pallas_call x1, Pallas kernels, local_terms(): pl.pallas_call(local_kernel, name='local_terms', grid=(steps,), in_specs=...  9.39 us
    pallas_call x1, Pallas kernels, to_send(): pl.pallas_call(send_kernel, name='to_send', grid=(WIDTH // n,), in_specs=...  7.61 us
  transfers between devices with their start and end apart: 10, of which 3 were waited for; matrix products, arithmetic and copies ran while one was open for 1% of the time, Pallas kernels for 17%

profile of v1, /device:TPU:51, one launch (start us, length us, event | category | flops | bytes accessed | tf_op | source)
XLA Modules:
  0.0 330.5 jit_solution(13314554864416158641)
XLA Ops:
  0.0 0.0 copy-start
  0.0 0.0 copy-start.13
  0.0 2.4 constant_dynamic-slice_fusion
  2.5 1.0 collective-permute-start.1
  3.5 0.3 collective-permute-start.2
  3.8 0.8 collective-permute-start.3
  4.6 0.8 slice.3
  5.5 3.0 collective-permute-start
  8.5 0.0 copy-done.16
  8.5 0.1 copy.24.ld_ref
  8.6 0.1 copy.25.ws_ref
  8.7 41.2 %collective-permute-done.qb_ref.kb_ref.vb_ref = bf16[8,4096]{1,0:T(8,128)(2,1)S(1)} collective-permute-done((bf16[8,4096]{1,0:T(8,128)(2,1)S(1)}, bf16[8,4096]{1,0:T(8,128)(2,1)S(1)}, u32[]{:S(2)}, u32[]{:S(2)}) %collective-permute-start) | collective-permute-done | bytes 65568 | tf_op jit(solution)/shard_map/ppermute | solution.py:562
  49.9 1.2 copy-done.9
  51.1 9.4 %local_terms.1 = (bf16[16,256,128]{2,1,0:T(8,128)(2,1)S(1)}, bf16[16,128,128]{2,1,0:T(8,128)(2,1)S(1)}, f32[16,128,128]{2,1,0:T(8,128)S(1)}) custom-call(bf16[128,4096]{1,0:T(8,128)(2,1)S(1)} %copy-done.9, bf16[128,4096]{1,0:T(8,128)(2,1)S(1)} %copy-done.9, bf16[128,4096]{1,0:T(8,128)(2,1)S(1)} %copy-done.9, ...), custom_call_target="tpu_custom_call" | custom-call | flops 8000000000 | bytes 6000000 | tf_op jit(solution)/shard_map/local_terms/pallas_call | solution.py:147
  60.5 0.0 collective-permute-done.1.a1
  60.5 2.3 collective-permute-start.4
  62.8 0.0 collective-permute-done.2.a2
  62.8 0.1 collective-permute-start.5
  62.9 0.0 collective-permute-done.3.a3
  62.9 0.4 collective-permute-start.6
  63.4 0.0 copy-start.10
  63.4 41.5 %scan_states.1.starts = bf16[16,128,128]{2,1,0:T(8,128)(2,1)S(1)} custom-call(bf16[16,256,128]{2,1,0:T(8,128)(2,1)S(1)} %get-tuple-element.17.maps), custom_call_target="tpu_custom_call" | custom-call | flops 30000001024 | bytes 4000000 | tf_op jit(solution)/shard_map/scan_states/pallas_call | solution.py:303
  104.9 0.0 collective-permute-done.4.b1
  104.9 0.0 collective-permute-done.5.b2
  105.0 0.0 collective-permute-done.6.b3
  105.0 1.2 copy-done.3
  106.2 3.4 %mix.1 = (bf16[128,2048]{1,0:T(8,128)(2,1)S(1)}, bf16[128,2048]{1,0:T(8,128)(2,1)S(1)}) custom-call(bf16[16,128,128]{2,1,0:T(8,128)(2,1)S(1)} %get-tuple-element.15.reads, f32[16,128,128]{2,1,0:T(8,128)S(1)} %get-tuple-element.16.offs, bf16[16,128,128]{2,1,0:T(8,128)(2,1)S(1)} %scan_states.1.starts, bf16[128,2048]{1,0:T(8,128)(2,1)S(1)} %copy-done.5, ...), custom_call_target="tpu_custom_call" | custom-call | flops 2000000000 | bytes 12000000 | tf_op jit(solution)/shard_map/mix/pallas_call | solution.py:375
  109.7 1.2 collective-permute-start.7
  110.9 0.3 collective-permute-start.8
  111.1 1.4 collective-permute-done.8
  112.5 0.1 copy.26.ids_ref
  112.6 4.3 %slots.1.sel_ref = bf16[256,1536]{1,0:T(8,128)(2,1)S(1)} custom-call(s32[256,10]{1,0:T(8,128)S(1)} %copy.26.ids_ref, s32[8,1536]{1,0:T(8,128)S(1)} %copy-done.7), custom_call_target="tpu_custom_call" | custom-call | flops 200000000 | bytes 1000000 | tf_op jit(solution)/shard_map/slots/pallas_call | solution.py:421
  116.9 0.0 collective-permute-done.7.other
  116.9 0.0 copy-start.12
  116.9 1.2 copy-done.12
  118.1 7.6 %to_send.1 = (bf16[1536,2048]{1,0:T(8,128)(2,1)S(1)}, bf16[256,1536]{1,0:T(8,128)(2,1)S(1)}, bf16[256,1536]{1,0:T(8,128)(2,1)S(1)}) custom-call(bf16[128,2048]{1,0:T(8,128)(2,1)S(1)} %get-tuple-element.19.own, bf16[128,2048]{1,0:T(8,128)(2,1)} %collective-permute-done.7.other, bf16[256,1536]{1,0:T(8,128)(2,1)S(1)} %slots.1.sel_ref, ...), custom_call_target="tpu_custom_call" | custom-call | flops 2000000000 | bytes 10000000 | tf_op jit(solution)/shard_map/to_send/pallas_call | solution.py:466
  125.8 0.0 copy-start.11
  125.8 80.4 %all_to_all.10 = bf16[64,24,2048]{2,1,0:T(8,128)(2,1)} all-to-all(bf16[64,24,2048]{2,1,0:T(8,128)(2,1)S(1)} %bitcast.29), channel_id=1, replica_groups=mesh['ctx_0'=4,'ctx_1'=4,'ctx_2'=2,'exp'=4] {'ctx_0','ctx_1','exp'}, dimensions={0} | all-to-all | bytes 12582912 | tf_op jit(solution)/shard_map/all_to_all | solution.py:521
  206.2 26.6 %experts.1 = bf16[1536,2048]{1,0:T(8,128)(2,1)} custom-call(bf16[1536,2048]{1,0:T(8,128)(2,1)} %bitcast.33, bf16[2,2048,512]{2,1,0:T(8,128)(2,1)S(1)} %copy-done.11, bf16[2,2048,512]{2,1,0:T(8,128)(2,1)} %up_ref.1, bf16[2,512,2048]{2,1,0:T(8,128)(2,1)} %down_ref.1), custom_call_target="tpu_custom_call" | custom-call | flops 20000000000 | bytes 24000000 | tf_op jit(solution)/shard_map/experts/pallas_call | solution.py:506
  232.8 82.0 %all_to_all.11 = bf16[64,24,2048]{2,1,0:T(8,128)(2,1)S(1)} all-to-all(bf16[64,24,2048]{2,1,0:T(8,128)(2,1)} %bitcast.34), channel_id=1, replica_groups=mesh['ctx_0'=4,'ctx_1'=4,'ctx_2'=2,'exp'=4] {'ctx_0','ctx_1','exp'}, dimensions={0} | all-to-all | bytes 12582912 | tf_op jit(solution)/shard_map/all_to_all | solution.py:521
  314.7 5.7 %gathered.1 = (f32[128,2048]{1,0:T(8,128)S(1)}, f32[128,2048]{1,0:T(8,128)S(1)}) custom-call(bf16[1536,2048]{1,0:T(8,128)(2,1)S(1)} %bitcast.30, bf16[256,1536]{1,0:T(8,128)(2,1)S(1)} %get-tuple-element.21.high_ref, bf16[256,1536]{1,0:T(8,128)(2,1)S(1)} %get-tuple-element.22.low_ref), custom_call_target="tpu_custom_call" | custom-call | flops 3000000000 | bytes 9000000 | tf_op jit(solution)/shard_map/gathered/pallas_call | solution.py:536
  320.4 1.0 copy-done.4
  321.4 2.0 collective-permute-start.9
  323.4 0.2 fusion.3
  323.6 0.5 fusion.8
  324.1 1.6 collective-permute-done.9
  325.6 1.0 copy-done.15
  326.6 3.9 %add_convert_fusion = bf16[128,2048]{1,0:T(8,128)(2,1)} fusion(f32[128,2048]{1,0:T(8,128)} %copy-done.15, f32[128,2048]{1,0:T(8,128)} %copy-done.4, bf16[128,2048]{1,0:T(8,128)(2,1)S(1)} %get-tuple-element.18, bf16[512,2048]{1,0:T(8,128)(2,1)S(1)} %copy-done, f32[128,512]{1,0:T(8,128)S(1)} %fusion.8, bf16[128,2048]{1,0:T(8,128)(2,1)S(1)} %get-tuple-element.19.own, ...), kind=kOutput, calls=%fused_computation.6 | convolution fusion | flops 538836992 | bytes 8126976 | tf_op jit(solution)/shard_map/dot_general | solution.py:589
  (31 shorter events, 0.1 us)
Async XLA Ops:
  0.0 326.6 %copy-start = (bf16[512,2048]{1,0:T(8,128)(2,1)S(1)}, bf16[512,2048]{1,0:T(8,128)(2,1)}, u32[]{:S(2)}) copy-start(bf16[512,2048]{1,0:T(8,128)(2,1)} %param.35) | copy-start | bytes 6291460
  0.0 8.5 %copy-start.16 = (f32[128,16]{0,1:T(8,128)S(1)}, f32[128,16]{0,1:T(8,128)}, u32[]{:S(2)}) copy-start(f32[128,16]{0,1:T(8,128)} %param.22) | copy-start | bytes 24580
  0.0 8.6 %copy-start.17 = (f32[128,16]{0,1:T(8,128)S(1)}, f32[128,16]{0,1:T(8,128)}, u32[]{:S(2)}) copy-start(f32[128,16]{0,1:T(8,128)} %param.23) | copy-start | bytes 24580
  0.0 49.9 %copy-start.13 = (f32[4,4096]{1,0:T(4,128)S(1)}, f32[4,4096]{1,0:T(4,128)}, u32[]{:S(2)}) copy-start(f32[4,4096]{1,0:T(4,128)} %vw_ref.1) | copy-start | bytes 196612
  2.5 58.1 %collective-permute-start.1 = (bf16[1024,512]{1,0:T(8,128)(2,1)}, bf16[1024,512]{1,0:T(8,128)(2,1)S(1)}, u32[]{:S(2)}, u32[]{:S(2)}) collective-permute-start(bf16[1024,512]{1,0:T(8,128)(2,1)} %constant_dynamic-slice_fusion), channel_id=1, source_target_pairs={{0,1},{1,2},{2,3},{3,0},{4,5},{5,6},{6,7},{7,4},{8,9},{9,10},{10,1... | collective-permute-start | bytes 3145736 | tf_op jit(solution)/shard_map/ppermute | solution.py:568
  3.5 59.4 %collective-permute-start.2 = (bf16[1024,512]{1,0:T(8,128)(2,1)}, bf16[1024,512]{1,0:T(8,128)(2,1)}, u32[]{:S(2)}, u32[]{:S(2)}) collective-permute-start(bf16[1024,512]{1,0:T(8,128)(2,1)} %constant_dynamic-slice_fusion), channel_id=1, source_target_pairs={{0,2},{1,3},{2,0},{3,1},{4,6},{5,7},{6,4},{7,5},{8,10},{9,11},{10,... | collective-permute-start | bytes 3145736 | tf_op jit(solution)/shard_map/ppermute | solution.py:568
  3.8 59.1 %collective-permute-start.3 = (bf16[1024,512]{1,0:T(8,128)(2,1)}, bf16[1024,512]{1,0:T(8,128)(2,1)}, u32[]{:S(2)}, u32[]{:S(2)}) collective-permute-start(bf16[1024,512]{1,0:T(8,128)(2,1)} %constant_dynamic-slice_fusion), channel_id=1, source_target_pairs={{0,3},{1,0},{2,1},{3,2},{4,7},{5,4},{6,5},{7,6},{8,11},{9,8},{10,9... | collective-permute-start | bytes 3145736 | tf_op jit(solution)/shard_map/ppermute | solution.py:568
  5.5 44.4 %collective-permute-start = (bf16[8,4096]{1,0:T(8,128)(2,1)S(1)}, bf16[8,4096]{1,0:T(8,128)(2,1)S(1)}, u32[]{:S(2)}, u32[]{:S(2)}) collective-permute-start(bf16[8,4096]{1,0:T(8,128)(2,1)S(1)} %slice.3), channel_id=1, source_target_pairs={{0,1},{1,2},{2,3},{3,4},{4,5},{5,6},{6,7},{7,8},{8,9},{9,10},{10,1... | collective-permute-start | bytes 196616 | tf_op jit(solution)/shard_map/ppermute | solution.py:562
  49.9 1.2 copy-start.9
  60.5 44.4 %copy-start.2 = (bf16[1024,512]{1,0:T(8,128)(2,1)}, bf16[1024,512]{1,0:T(8,128)(2,1)S(1)}, u32[]{:S(2)}) copy-start(bf16[1024,512]{1,0:T(8,128)(2,1)S(1)} %collective-permute-done.1.a1) | copy-start | bytes 3145732
  60.5 44.4 %collective-permute-start.4 = (bf16[1024,512]{1,0:T(8,128)(2,1)S(1)}, bf16[1024,512]{1,0:T(8,128)(2,1)S(1)}, u32[]{:S(2)}, u32[]{:S(2)}) collective-permute-start(bf16[1024,512]{1,0:T(8,128)(2,1)S(1)} %collective-permute-done.1.a1), channel_id=1, source_target_pairs={{0,4},{4,0},{1,5},{5,1},{2,6},{6,2},{3,7},{7,3},{8,12},{12,8},{9,1... | collective-permute-start | bytes 3145736 | tf_op jit(solution)/shard_map/ppermute | solution.py:553
  62.8 42.1 %collective-permute-start.5 = (bf16[1024,512]{1,0:T(8,128)(2,1)}, bf16[1024,512]{1,0:T(8,128)(2,1)S(1)}, u32[]{:S(2)}, u32[]{:S(2)}) collective-permute-start(bf16[1024,512]{1,0:T(8,128)(2,1)} %collective-permute-done.2.a2), channel_id=1, source_target_pairs={{0,4},{4,0},{1,5},{5,1},{2,6},{6,2},{3,7},{7,3},{8,12},{12,8},{9,1... | collective-permute-start | bytes 3145736 | tf_op jit(solution)/shard_map/ppermute | solution.py:553
  62.9 42.0 %collective-permute-start.6 = (bf16[1024,512]{1,0:T(8,128)(2,1)}, bf16[1024,512]{1,0:T(8,128)(2,1)S(1)}, u32[]{:S(2)}, u32[]{:S(2)}) collective-permute-start(bf16[1024,512]{1,0:T(8,128)(2,1)} %collective-permute-done.3.a3), channel_id=1, source_target_pairs={{0,4},{4,0},{1,5},{5,1},{2,6},{6,2},{3,7},{7,3},{8,12},{12,8},{9,1... | collective-permute-start | bytes 3145736 | tf_op jit(solution)/shard_map/ppermute | solution.py:553
  63.4 41.6 %copy-start.1 = (bf16[2048,512]{1,0:T(8,128)(2,1)S(1)}, bf16[2048,512]{1,0:T(8,128)(2,1)}, u32[]{:S(2)}) copy-start(bf16[2048,512]{1,0:T(8,128)(2,1)} %own.1) | copy-start | bytes 6291460
  63.4 41.6 %copy-start.5 = (bf16[128,2048]{1,0:T(8,128)(2,1)S(1)}, bf16[128,2048]{1,0:T(8,128)(2,1)}, u32[]{:S(2)}) copy-start(bf16[128,2048]{1,0:T(8,128)(2,1)} %gate_ref.2) | copy-start | bytes 1572868
  63.4 41.6 %copy-start.6 = (bf16[128,2048]{1,0:T(8,128)(2,1)S(1)}, bf16[128,2048]{1,0:T(8,128)(2,1)}, u32[]{:S(2)}) copy-start(bf16[128,2048]{1,0:T(8,128)(2,1)} %res_ref.1) | copy-start | bytes 1572868
  63.4 41.6 %copy-start.8 = (f32[2048]{0:T(1024)S(1)}, f32[2048]{0:T(1024)}, u32[]{:S(2)}) copy-start(f32[2048]{0:T(1024)} %param.27) | copy-start | bytes 24580
  63.4 41.6 %copy-start.10 = (f32[128]{0:T(128)S(1)}, f32[128]{0:T(128)}, u32[]{:S(2)}) copy-start(f32[128]{0:T(128)} %param.25) | copy-start | bytes 1540
  105.0 1.2 copy-start.3
  106.2 4.6 %copy-start.18 = (s32[128,10]{0,1:T(8,128)S(1)}, s32[128,10]{0,1:T(8,128)}, u32[]{:S(2)}) copy-start(s32[128,10]{0,1:T(8,128)} %param.29) | copy-start | bytes 15364
  106.2 6.4 %copy-start.7 = (s32[8,1536]{1,0:T(8,128)S(1)}, s32[8,1536]{1,0:T(8,128)}, u32[]{:S(2)}) copy-start(s32[8,1536]{1,0:T(8,128)} %constant.18.clone.table_ref) | copy-start | bytes 147460
  109.7 7.2 %collective-permute-start.7 = (bf16[128,2048]{1,0:T(8,128)(2,1)S(1)}, bf16[128,2048]{1,0:T(8,128)(2,1)}, u32[]{:S(2)}, u32[]{:S(2)}) collective-permute-start(bf16[128,2048]{1,0:T(8,128)(2,1)S(1)} %get-tuple-element.19.own), channel_id=1, source_target_pairs={{0,4},{4,0},{1,5},{5,1},{2,6},{6,2},{3,7},{7,3},{8,12},{12,8},{9,1... | collective-permute-start | bytes 1572872 | tf_op jit(solution)/shard_map/ppermute | solution.py:553
  110.9 1.7 collective-permute-start.8
  116.9 1.2 copy-start.12
  125.8 80.4 %copy-start.11 = (bf16[2,2048,512]{2,1,0:T(8,128)(2,1)S(1)}, bf16[2,2048,512]{2,1,0:T(8,128)(2,1)}, u32[]{:S(2)}) copy-start(bf16[2,2048,512]{2,1,0:T(8,128)(2,1)} %gate_ref.3) | copy-start | bytes 12582916
  314.7 8.6 %copy-start.19 = (bf16[2048]{0:T(1024)(128)(2,1)S(1)}, bf16[2048]{0:T(1024)(128)(2,1)}, u32[]{:S(2)}) copy-start(bf16[2048]{0:T(1024)(128)(2,1)} %param.36) | copy-start | bytes 12292
  314.7 8.9 %copy-start.14 = (bf16[2048,512]{1,0:T(8,128)(2,1)S(1)}, bf16[2048,512]{1,0:T(8,128)(2,1)}, u32[]{:S(2)}) copy-start(bf16[2048,512]{1,0:T(8,128)(2,1)} %param.33) | copy-start | bytes 6291460
  320.4 1.0 copy-start.4
  321.4 4.2 %collective-permute-start.9 = (f32[128,2048]{1,0:T(8,128)S(1)}, f32[128,2048]{1,0:T(8,128)S(1)}, u32[]{:S(2)}, u32[]{:S(2)}) collective-permute-start(f32[128,2048]{1,0:T(8,128)S(1)} %get-tuple-element.24), channel_id=1, source_target_pairs={{0,4},{4,0},{1,5},{5,1},{2,6},{6,2},{3,7},{7,3},{8,12},{12,8},{9,1... | collective-permute-start | bytes 3145736 | tf_op jit(solution)/shard_map/ppermute | solution.py:553
  325.6 1.0 copy-start.15

commit v2 on v1

--- a/solution.py
+++ b/solution.py
@@ -15,7 +15,6 @@
 WIDTH = 2048
 EXPERTS = 256
 AXES = ("ctx_0", "ctx_1", "ctx_2", "exp")
-SAME_CORE = ("ctx_0", "ctx_1", "exp")
 PEERS = 64
 SLOTS = 4 * CAP
 SENT = PEERS * SLOTS
@@ -176,8 +175,9 @@
 
 
 def scan_kernel(
-    maps, starts, got1, pre1, tot1, got2, pre2, tot2, got3, st4, got4, st5, got5,
+    maps, weight, starts, wall, got1, pre1, tot1, got2, pre2, tot2, got3, st4, got4, st5, got5,
     send1, recv1, send2, recv2, send3, recv3, send4, recv4, send5, recv5,
+    sendw1, recvw1, sendw2, recvw2, sendw3, recvw3,
 ):
     z, x, c, y = (lax.axis_index(a) for a in AXES)
     place = 2 * x + c
@@ -212,6 +212,15 @@
             send(maps.at[pl.ds(4 * other, 4)], got1.at[y], send1.at[j], recv1.at[j], at(j, "y"))
         )
     got1[y] = maps[pl.ds(4 * y, 4)]
+    first = []
+    for j in range(1, 4):
+        for part, quarter in ((0, x), (1, z)):
+            first.append(
+                send(
+                    weight.at[part, quarter, c], wall.at[y, part, quarter, c],
+                    sendw1.at[j, part], recvw1.at[j, part], at(j, "y"),
+                )
+            )
     for copy in copies:
         copy.wait_recv()
     for h in range(4):
@@ -273,6 +282,20 @@
             send(st4.at[other], got4.at[x, rows_here], send4.at[j], recv4.at[j], at(j, "p"))
         )
     got4[x, rows_here, :] = st4[place]
+    for copy in first:
+        copy.wait_recv()
+    second = []
+    for k in range(1, 4):
+        for j in range(1, 4):
+            other = lax.rem(y + j, 4)
+            for part, quarter, device in (
+                (0, x, {"ctx_1": lax.rem(x + k, 4)}),
+                (1, z, {"ctx_0": lax.rem(z + k, 4)}),
+            ):
+                held = wall.at[other, part, quarter, c]
+                second.append(
+                    send(held, held, sendw2.at[k, j, part], recvw2.at[k, j, part], device)
+                )
     for copy in copies:
         copy.wait_recv()
     for h in range(4):
@@ -294,18 +317,30 @@
         copy.wait_recv()
     for m in range(4):
         starts[4 * m : 4 * m + 4] = got5[m]
+    for copy in second:
+        copy.wait_recv()
+    third = []
+    for j in range(1, 4):
+        held = wall.at[lax.rem(y + j, 4), :, :, c]
+        third.append(send(held, held, sendw3.at[j], recvw3.at[j], {"ctx_2": 1 - c}))
+    for copy in third:
+        copy.wait_recv()
     for copy in started:
         copy.wait_send()
 
 
-def scan_states(maps):
+def scan_states(maps, out_weight):
     dma = pltpu.SemaphoreType.DMA
+    cut = (2, 4, 2, WIDTH // 16, WIDTH // 4)
     return pl.pallas_call(
         scan_kernel,
         name="scan_states",
-        in_specs=[VM],
-        out_specs=VM,
-        out_shape=jax.ShapeDtypeStruct((VHEADS, HEAD, HEAD), BF16),
+        in_specs=[VM, ANY],
+        out_specs=[VM, ANY],
+        out_shape=[
+            jax.ShapeDtypeStruct((VHEADS, HEAD, HEAD), BF16),
+            jax.ShapeDtypeStruct((4, *cut), BF16),
+        ],
         scratch_shapes=[
             pltpu.VMEM((4, 4, 2 * HEAD, HEAD), BF16),
             pltpu.VMEM((3, 4, 2 * HEAD, HEAD), BF16),
@@ -320,6 +355,7 @@
             pltpu.VMEM((4, 4, HEAD, HEAD), BF16),
             dma((4,)), dma((4,)), dma((8, 2)), dma((8, 2)), dma((4,)), dma((4,)),
             dma((8,)), dma((8,)), dma((4,)), dma((4,)),
+            dma((4, 2)), dma((4, 2)), dma((4, 4, 2)), dma((4, 4, 2)), dma((4,)), dma((4,)),
         ],
         compiler_params=pltpu.CompilerParams(
             collective_id=0, has_side_effects=True, vmem_limit_bytes=32 << 20
@@ -327,24 +363,18 @@
         cost_estimate=pl.CostEstimate(
             flops=30_000_000_000, bytes_accessed=4_000_000, transcendentals=0
         ),
-    )(maps)
+    )(maps, out_weight.reshape(cut))
 
 
 def mix_kernel(
-    reads, offs, starts, gate_ref, gain_ref, res_ref, post_ref, own, a1, a2, a3, b1, b2, b3,
+    reads, offs, starts, gate_ref, gain_ref, res_ref, post_ref, own, wall,
     after_ref, routed_ref, weights, normed, total, sems,
 ):
-    c, y = lax.axis_index("ctx_2"), lax.axis_index("exp")
-    half = WIDTH // 2
-    mine = pl.ds(pl.multiple_of(half * c, half), half)
-    theirs = pl.ds(pl.multiple_of(half * (1 - c), half), half)
+    y = lax.axis_index("exp")
     loads = [[pltpu.make_async_copy(own, weights.at[0], sems.at[0])]]
-    for j, (a, b) in enumerate(((a1, b1), (a2, b2), (a3, b3)), 1):
+    for j in range(1, 4):
         loads.append(
-            [
-                pltpu.make_async_copy(a, weights.at[j, mine], sems.at[2 * j - 1]),
-                pltpu.make_async_copy(b, weights.at[j, theirs], sems.at[2 * j]),
-            ]
+            [pltpu.make_async_copy(wall.at[lax.rem(y + j, 4)], weights.at[j], sems.at[j])]
         )
     for group in loads:
         for load in group:
@@ -359,7 +389,7 @@
     for j in range(4):
         for load in loads[j]:
             load.wait()
-        block = lax.rem(y + 4 - j, 4)
+        block = lax.rem(y + j, 4)
         here = pl.ds(pl.multiple_of(columns * block, columns), columns)
         total[:, here] = nn(normed[...], weights[j])
     after = (res_ref[...].astype(F32) + total[...]).astype(BF16)
@@ -370,48 +400,71 @@
     ).astype(BF16)
 
 
-def mix(reads, offs, starts, gate, gain, residual, post, own, near, far):
+def mix(reads, offs, starts, gate, gain, residual, post, own, wall):
     shape = jax.ShapeDtypeStruct((ROWS, WIDTH), BF16)
     return pl.pallas_call(
         mix_kernel,
         name="mix",
-        in_specs=[VM] * 7 + [ANY] * 7,
+        in_specs=[VM] * 7 + [ANY] * 2,
         out_specs=[VM, VM],
         out_shape=[shape, shape],
         scratch_shapes=[
             pltpu.VMEM((4, WIDTH, WIDTH // 4), BF16),
             pltpu.VMEM((ROWS, WIDTH), BF16),
             pltpu.VMEM((ROWS, WIDTH), F32),
-            pltpu.SemaphoreType.DMA((7,)),
+            pltpu.SemaphoreType.DMA((4,)),
         ],
         compiler_params=pltpu.CompilerParams(vmem_limit_bytes=40 << 20),
         cost_estimate=pl.CostEstimate(
             flops=2_000_000_000, bytes_accessed=12_000_000, transcendentals=300_000
         ),
-    )(reads, offs, starts, gate, gain, residual, post, own, *near, *far)
+    )(reads, offs, starts, gate, gain, residual, post, own, wall.reshape(4, WIDTH, WIDTH // 4))
+
+
+def distance(group, i):
+    dx = lax.rem(i, 4)
+    dy = lax.rem(dx + lax.rem(group, 4), 4)
+    dz = lax.rem(dx + 2 * (i // 4) + group // 4, 4)
+    return dz, dx, dy
 
 
 LANES = np.arange(SENT)
 PEER, INSIDE = LANES // SLOTS, LANES % SLOTS
-EXPERT_OF = 2 * (PEER // 4 * 8 + PEER % 4) + INSIDE // (2 * CAP)
+NEAR = PEER % 8
 TABLE = np.stack(
-    [EXPERT_OF, INSIDE % (2 * CAP) // CAP, INSIDE % CAP] + [np.zeros(SENT, np.int64)] * 5
+    [
+        (NEAR + 2 * (NEAR // 4) + PEER // 32) % 4,
+        NEAR % 4,
+        (NEAR + PEER // 8) % 4,
+        INSIDE // (2 * CAP),
+        INSIDE % (2 * CAP) // CAP,
+        INSIDE % CAP,
+        0 * LANES,
+        0 * LANES,
+    ]
 ).astype(np.int32)
 
 
+def wanted_experts(table_ref, lanes=slice(None)):
+    z, x, c, y = (lax.axis_index(a) for a in AXES)
+    there = ((table_ref[0:1, lanes] + z) & 3) * 32 + ((table_ref[1:2, lanes] + x) & 3) * 8
+    there = there + c * 4 + ((table_ref[2:3, lanes] + y) & 3)
+    return 2 * there + table_ref[3:4, lanes]
+
+
 def slot_kernel(ids_ref, table_ref, sel_ref):
-    c = lax.axis_index("ctx_2")
-    wanted = table_ref[0:1, :] + 8 * c
-    source, slot = table_ref[1:2, :], table_ref[2:3, :]
+    wanted = wanted_experts(table_ref)
+    source, slot = table_ref[4:5, :], table_ref[5:6, :]
     rows = lax.broadcasted_iota(jnp.int32, (ROWS, ROWS), 0)
     cols = lax.broadcasted_iota(jnp.int32, (ROWS, ROWS), 1)
     earlier = (rows > cols).astype(BF16)
     for half in range(2):
         part = slice(half * ROWS, (half + 1) * ROWS)
         ids = ids_ref[part, :]
-        hit = (ids[:, 0:1] == wanted) & (source == half)
+        aim = jnp.where(source == half, wanted, -1)
+        hit = ids[:, 0:1] == aim
         for k in range(1, TOP):
-            hit = hit | ((ids[:, k : k + 1] == wanted) & (source == half))
+            hit = hit | (ids[:, k : k + 1] == aim)
         marks = hit.astype(F32)
         rank = nn(earlier, marks.astype(BF16))
         sel_ref[part, :] = jnp.where(rank == slot.astype(F32), marks, 0.0).astype(BF16)
@@ -431,122 +484,199 @@
     )(ids, jnp.asarray(TABLE))
 
 
-def send_kernel(own, other, sel_ref, ids_ref, table_ref, router, out_ref, high_ref, low_ref):
-    rows = jnp.concatenate([own[...], other[...]], axis=0)
-
-    @pl.when(pl.program_id(0) == 0)
-    def _():
-        logits = nn(rows, router[...])
-        lane = lax.broadcasted_iota(jnp.int32, (2 * ROWS, EXPERTS), 1)
-        ids = ids_ref[...]
-        hit = ids[:, 0:1] == lane
-        for k in range(1, TOP):
-            hit = hit | (ids[:, k : k + 1] == lane)
-        chosen = jnp.where(hit, jnp.exp(jnp.where(hit, logits, 0.0)), 0.0)
-        gates = chosen / jnp.sum(chosen, axis=1, keepdims=True)
-        wanted = table_ref[0:1, :] + 8 * lax.axis_index("ctx_2")
+GROUPS, EACH = 8, 8
+BUILT = 2 * EACH * SLOTS
+
+
+def moe_kernel(
+    routed, after, sel, ids_ref, table_ref, switch, router, s_gate, s_up, s_down, gate, up, down,
+    out_ref, rows2, out_buf, in_buf, back_buf, high, low, total, swap, theirs,
+    v_router, v_sgate, v_sup, v_sdown, v_gate, v_up, v_down,
+    load_sems, send_x, recv_x, send1, recv1, send2, recv2, send_y, recv_y,
+):
+    z, x, c, y = (lax.axis_index(a) for a in AXES)
+    partner = {"ctx_2": 1 - c}
+    barrier = pltpu.get_barrier_semaphore()
+
+    def peer(group, i, sign):
+        dz, dx, dy = distance(group, i)
+        return {
+            "ctx_0": lax.rem(z + 4 + sign * dz, 4),
+            "ctx_1": lax.rem(x + 4 + sign * dx, 4),
+            "exp": lax.rem(y + 4 + sign * dy, 4),
+        }
+
+    def greet(k, _):
+        pl.semaphore_signal(
+            barrier, inc=1, device_id=peer(k // EACH, lax.rem(k, EACH), 1), device_id_type=MESH
+        )
+        return 0
+
+    lax.fori_loop(1, PEERS, greet, 0)
+    pl.semaphore_signal(barrier, inc=1, device_id=partner, device_id_type=MESH)
+    loads = [
+        pltpu.make_async_copy(src, dst, load_sems.at[k])
+        for k, (src, dst) in enumerate(
+            (
+                (router, v_router), (s_gate, v_sgate), (s_up, v_sup), (s_down, v_sdown),
+                (gate, v_gate), (up, v_up), (down, v_down),
+            )
+        )
+    ]
+    for load in loads:
+        load.start()
+    pl.semaphore_wait(barrier, PEERS)
+
+    both = pltpu.make_async_remote_copy(
+        src_ref=routed, dst_ref=rows2.at[ROWS : 2 * ROWS], send_sem=send_x, recv_sem=recv_x,
+        device_id=partner, device_id_type=MESH,
+    )
+    both.start()
+    rows2[0:ROWS, :] = routed[...]
+    both.wait_recv()
+
+    def remote(src, dst, s, r, device):
+        return pltpu.make_async_remote_copy(
+            src_ref=src, dst_ref=dst, send_sem=s, recv_sem=r, device_id=device, device_id_type=MESH
+        )
+
+    def dispatch(group, begin):
+        def one(i, _):
+            g = group * EACH + i
+            remote(
+                out_buf.at[g], in_buf.at[g], send1.at[group], recv1.at[group], peer(group, i, 1)
+            ).start()
+            return 0
+
+        lax.fori_loop(begin, EACH, one, 0)
+
+    def give_back(group, begin):
+        def one(i, _):
+            g = group * EACH + i
+            remote(
+                in_buf.at[g], back_buf.at[g], send2.at[group], recv2.at[group], peer(group, i, -1)
+            ).start()
+            return 0
+
+        lax.fori_loop(begin, EACH, one, 0)
+
+    for p in range(GROUPS // 2):
+        lanes = slice(p * BUILT, (p + 1) * BUILT)
+        built = tn(sel[:, lanes], rows2[...]).astype(BF16)
+        out_buf[2 * p * EACH : 2 * (p + 1) * EACH] = built.reshape(2 * EACH, SLOTS, WIDTH)
+        dispatch(2 * p, 0 if p else 1)
+        dispatch(2 * p + 1, 0)
+        if p == 0:
+            pltpu.make_async_copy(out_buf.at[0], in_buf.at[0], recv1.at[0]).start()
+
+    loads[0].wait()
+    logits = nn(rows2[...], v_router[...])
+    lane = lax.broadcasted_iota(jnp.int32, (2 * ROWS, EXPERTS), 1)
+    ids = ids_ref[...]
+    hit = ids[:, 0:1] == lane
+    for k in range(1, TOP):
+        hit = hit | (ids[:, k : k + 1] == lane)
+    chosen = jnp.where(hit, jnp.exp(jnp.where(hit, logits, 0.0)), 0.0)
+    gates = chosen / jnp.sum(chosen, axis=1, keepdims=True)
+    gates_high = gates.astype(BF16)
+    gates_low = (gates - gates_high.astype(F32)).astype(BF16)
+    for p in range(GROUPS // 2):
+        lanes = slice(p * BUILT, (p + 1) * BUILT)
         spread = (
-            lax.broadcasted_iota(jnp.int32, (EXPERTS, SENT), 0) == wanted
+            lax.broadcasted_iota(jnp.int32, (EXPERTS, BUILT), 0) == wanted_experts(table_ref, lanes)
         ).astype(BF16)
-        high = gates.astype(BF16)
-        low = (gates - high.astype(F32)).astype(BF16)
-        sel = sel_ref[...]
-        high_ref[...] = nn(high, spread).astype(BF16) * sel
-        low_ref[...] = nn(low, spread).astype(BF16) * sel
-
-    n = out_ref.shape[1]
-    here = pl.ds(pl.multiple_of(pl.program_id(0) * n, n), n)
-    cut = jnp.concatenate([own[:, here], other[:, here]], axis=0)
-    out_ref[...] = tn(sel_ref[...], cut).astype(BF16)
-
-
-def to_send(own, other, sel, ids, router):
-    n = 256
-    full = lambda *shape: pl.BlockSpec(shape, lambda s: (0,) * len(shape))
+        high[p] = nn(gates_high, spread).astype(BF16) * sel[:, lanes]
+        low[p] = nn(gates_low, spread).astype(BF16) * sel[:, lanes]
+
+    for load in loads[1:4]:
+        load.wait()
+    mine = routed[...]
+    hidden = (silu(nn(mine, v_sgate[...])) * nn(mine, v_sup[...])).astype(BF16)
+    open_ = jnp.sum(mine.astype(F32) * switch[...].astype(F32), axis=1, keepdims=True)
+    total[0:ROWS, :] = after[...].astype(F32) + nn(hidden, v_sdown[...]) / (1.0 + jnp.exp(-open_))
+    total[ROWS:, :] = jnp.zeros((ROWS, WIDTH), F32)
+
+    for load in loads[4:]:
+        load.wait()
+
+    def serve(group, begin):
+        here = pl.ds(group * EACH, EACH)
+        pltpu.make_async_copy(in_buf.at[here], in_buf.at[here], recv1.at[group]).wait()
+        n = EACH * SLOTS
+        rows = in_buf[here].reshape(n, WIDTH)
+        inside = lax.rem(lax.broadcasted_iota(jnp.int32, (n, 1), 0), SLOTS)
+        result = None
+        for e in range(2):
+            hidden = silu(nn(rows, v_gate[e])) * nn(rows, v_up[e])
+            hidden = jnp.where((inside >= 2 * CAP) == bool(e), hidden, 0.0).astype(BF16)
+            part = nn(hidden, v_down[e])
+            result = part if result is None else result + part
+        in_buf[here] = result.astype(BF16).reshape(EACH, SLOTS, WIDTH)
+
+    serve(0, 1)
+    pltpu.make_async_copy(in_buf.at[0], back_buf.at[0], recv2.at[0]).start()
+    give_back(0, 1)
+
+    def later(group, _):
+        serve(group, 0)
+        give_back(group, 0)
+        return 0
+
+    lax.fori_loop(1, GROUPS, later, 0)
+
+    for p in range(GROUPS // 2):
+        for group in (2 * p, 2 * p + 1):
+            here = pl.ds(group * EACH, EACH)
+            pltpu.make_async_copy(back_buf.at[here], back_buf.at[here], recv2.at[group]).wait()
+        rows = back_buf[2 * p * EACH : 2 * (p + 1) * EACH].reshape(BUILT, WIDTH)
+        total[...] += nn(high[p], rows) + nn(low[p], rows)
+
+    theirs[...] = total[ROWS:, :]
+    last = remote(theirs, swap, send_y, recv_y, partner)
+    last.start()
+    last.wait_recv()
+    out_ref[...] = (total[0:ROWS, :] + swap[...]).astype(BF16)
+
+    both.wait_send()
+    last.wait_send()
+    for group in range(GROUPS):
+        here = pl.ds(1, EACH - 1) if group == 0 else pl.ds(group * EACH, EACH)
+        pltpu.make_async_copy(out_buf.at[here], out_buf.at[here], send1.at[group]).wait()
+        pltpu.make_async_copy(in_buf.at[here], in_buf.at[here], send2.at[group]).wait()
+
+
+def experts(
+    routed, after, sel, ids, switch, router, s_gate, s_up, s_down, gate, up, down
+):
+    dma = pltpu.SemaphoreType.DMA
+    vmem = lambda a: pltpu.VMEM(a.shape, a.dtype)
+    slabs = pltpu.VMEM((PEERS, SLOTS, WIDTH), BF16)
+    weights = (router, s_gate, s_up, s_down, gate, up, down)
     return pl.pallas_call(
-        send_kernel,
-        name="to_send",
-        grid=(WIDTH // n,),
-        in_specs=[
-            full(ROWS, WIDTH), full(ROWS, WIDTH), full(2 * ROWS, SENT), full(2 * ROWS, TOP),
-            full(8, SENT), full(WIDTH, EXPERTS),
+        moe_kernel,
+        name="experts",
+        in_specs=[VM] * 6 + [ANY] * 7,
+        out_specs=VM,
+        out_shape=jax.ShapeDtypeStruct((ROWS, WIDTH), BF16),
+        scratch_shapes=[
+            pltpu.VMEM((2 * ROWS, WIDTH), BF16),
+            slabs, slabs, slabs,
+            pltpu.VMEM((GROUPS // 2, 2 * ROWS, BUILT), BF16),
+            pltpu.VMEM((GROUPS // 2, 2 * ROWS, BUILT), BF16),
+            pltpu.VMEM((2 * ROWS, WIDTH), F32),
+            pltpu.VMEM((ROWS, WIDTH), F32),
+            pltpu.VMEM((ROWS, WIDTH), F32),
+            *(vmem(w) for w in weights),
+            dma((7,)), dma, dma, dma((GROUPS,)), dma((GROUPS,)), dma((GROUPS,)), dma((GROUPS,)),
+            dma, dma,
         ],
-        out_specs=[
-            pl.BlockSpec((SENT, n), lambda s: (0, s)), full(2 * ROWS, SENT), full(2 * ROWS, SENT),
-        ],
-        out_shape=[
-            jax.ShapeDtypeStruct((SENT, WIDTH), BF16),
-            jax.ShapeDtypeStruct((2 * ROWS, SENT), BF16),
-            jax.ShapeDtypeStruct((2 * ROWS, SENT), BF16),
-        ],
-        compiler_params=pltpu.CompilerParams(vmem_limit_bytes=40 << 20),
+        compiler_params=pltpu.CompilerParams(
+            collective_id=1, has_side_effects=True, vmem_limit_bytes=62 << 20
+        ),
         cost_estimate=pl.CostEstimate(
-            flops=2_000_000_000, bytes_accessed=10_000_000, transcendentals=70_000
+            flops=60_000_000_000, bytes_accessed=30_000_000, transcendentals=2_000_000
         ),
-    )(own, other, sel, ids, jnp.asarray(TABLE), router)
-
-
-def expert_kernel(x_ref, gate_ref, up_ref, down_ref, out_ref):
-    x = x_ref[...]
-    n = x.shape[0]
-    inside = lax.rem(lax.broadcasted_iota(jnp.int32, (n, 1), 0), SLOTS)
-    total = None
-    for e in range(2):
-        hidden = silu(nn(x, gate_ref[e])) * nn(x, up_ref[e])
-        hidden = jnp.where((inside >= 2 * CAP) == bool(e), hidden, 0.0).astype(BF16)
-        part = nn(hidden, down_ref[e])
-        total = part if total is None else total + part
-    out_ref[...] = total.astype(BF16)
-
-
-def run_experts(received, gate, up, down):
-    n = SENT // 8
-    once = lambda a: pl.BlockSpec(a.shape, lambda s: (0, 0, 0), pipeline_mode=pl.Buffered(1))
-    rows = pl.BlockSpec((n, WIDTH), lambda s: (s, 0))
-    return pl.pallas_call(
-        expert_kernel,
-        name="experts",
-        grid=(SENT // n,),
-        in_specs=[rows, once(gate), once(up), once(down)],
-        out_specs=rows,
-        out_shape=jax.ShapeDtypeStruct((SENT, WIDTH), BF16),
-        compiler_params=pltpu.CompilerParams(vmem_limit_bytes=48 << 20),
-        cost_estimate=pl.CostEstimate(
-            flops=20_000_000_000, bytes_accessed=24_000_000, transcendentals=1_600_000
-        ),
-    )(received, gate, up, down)
-
-
-def exchange(x):
-    return lax.all_to_all(x, SAME_CORE, split_axis=0, concat_axis=0, tiled=True)
-
-
-def gather_kernel(back, high_ref, low_ref, mine_ref, theirs_ref):
-    rows = back[...]
-    both = nn(high_ref[...], rows) + nn(low_ref[...], rows)
-    mine_ref[...] = both[0:ROWS]
-    theirs_ref[...] = both[ROWS:]
-
-
-def gathered(back, high, low):
-    n = 256
-    full = lambda *shape: pl.BlockSpec(shape, lambda s: (0,) * len(shape))
-    part = pl.BlockSpec((ROWS, n), lambda s: (0, s))
-    shape = jax.ShapeDtypeStruct((ROWS, WIDTH), F32)
-    return pl.pallas_call(
-        gather_kernel,
-        name="gathered",
-        grid=(WIDTH // n,),
-        in_specs=[
-            pl.BlockSpec((SENT, n), lambda s: (0, s)), full(2 * ROWS, SENT), full(2 * ROWS, SENT),
-        ],
-        out_specs=[part, part],
-        out_shape=[shape, shape],
-        compiler_params=pltpu.CompilerParams(vmem_limit_bytes=32 << 20),
-        cost_estimate=pl.CostEstimate(
-            flops=3_000_000_000, bytes_accessed=9_000_000, transcendentals=0
-        ),
-    )(back, high, low)
+    )(routed, after, sel, ids, jnp.asarray(TABLE), switch, *weights)
 
 
 def from_other_core(a):
@@ -562,34 +692,19 @@
     before = lax.ppermute(
         mixed_qkv[ROWS - 8 :], AXES, [(k, k + 1) for k in range(count - 1)]
     )
-    half = WIDTH // 2
-    own_half = lax.dynamic_slice_in_dim(out_weight, lax.axis_index("ctx_2") * half, half, 0)
-    near = [
-        lax.ppermute(own_half, "exp", [(k, (k + j) % 4) for k in range(4)]) for j in (1, 2, 3)
-    ]
-    far = [from_other_core(a) for a in near]
-    maps, reads, offs = local_terms(mixed_qkv, before, conv_weight, log_decay, write_strength)
-    starts = scan_states(maps)
     ids = jnp.concatenate([expert_ids, from_other_core(expert_ids)], axis=0)
     sel = slots(ids)
+    before, sel = lax.optimization_barrier((before, sel))
+    maps, reads, offs = local_terms(mixed_qkv, before, conv_weight, log_decay, write_strength)
+    starts, wall = scan_states(maps, out_weight)
     after_mix, routed_in = mix(
         reads, offs, starts, output_gate, norm_gain.reshape(1, HEAD), residual,
-        post_gain.reshape(1, WIDTH), out_weight, near, far,
+        post_gain.reshape(1, WIDTH), out_weight, wall,
     )
-    outgoing, high, low = to_send(routed_in, from_other_core(routed_in), sel, ids, router_weight)
-    received = exchange(outgoing.reshape(PEERS, SLOTS, WIDTH)).reshape(SENT, WIDTH)
-    result = run_experts(received, expert_gate, expert_up, expert_down)
-    returned = exchange(result.reshape(PEERS, SLOTS, WIDTH)).reshape(SENT, WIDTH)
-    mine, theirs = gathered(returned, high, low)
-    shared_hidden = (
-        jax.nn.silu(jnp.dot(routed_in, shared_gate, preferred_element_type=F32))
-        * jnp.dot(routed_in, shared_up, preferred_element_type=F32)
-    ).astype(BF16)
-    switch_rows = jax.nn.sigmoid(jnp.dot(routed_in, shared_switch, preferred_element_type=F32))
-    shared_out = switch_rows[:, None] * jnp.dot(
-        shared_hidden, shared_down, preferred_element_type=F32
+    return experts(
+        routed_in, after_mix, sel, ids, shared_switch.reshape(1, WIDTH), router_weight,
+        shared_gate, shared_up, shared_down, expert_gate, expert_up, expert_down,
     )
-    return (after_mix.astype(F32) + shared_out + mine + from_other_core(theirs)).astype(BF16)
 
 
 def solution(mesh):

time: 335 us -> 290 us (0.87); the launches traced: 331 us -> 290 us
  Pallas kernels: 98.4 us -> 271 us
  blocking collectives: 162 us -> 0 us
  waiting for transfers between devices: 44.2 us -> 0.01 us
  starting transfers between devices: 11.4 us -> 3.57 us
  local copies, waits for them, and re-layouts: 9.26 us -> 14.5 us
  matrix products: 4.64 us -> 0 us
    pallas_call x5 -> x3, Pallas kernels: 84.8 us -> 259 us  [the longest x1 199 us: experts(): pl.pallas_call(moe_kernel, name='experts', in_specs=[VM] * 6 + [ANY] * 7,...]
    all_to_all x2 -> x0, blocking collectives: 162 us -> none  [exchange(): return lax.all_to_all(x, SAME_CORE, split_axis=0, concat_axis=0, tiled=True)]
    ppermute x1, waiting for transfers between devices: 41.2 us -> 0.01 us  [local(): lax.ppermute(mixed_qkv[ROWS - 8:], AXES, [(k, k + 1) for k in range(count...]
    unnamed x43 -> x29, local copies, waits for them, and re-layouts: 5.87 us -> 12.3 us
    ppermute x6 -> x1, starting transfers between devices: 6.22 us -> 0.68 us  [from_other_core(): return lax.ppermute(a, 'ctx_2', [(0, 1), (1, 0)])]
    dot_general x3 -> x0, matrix products: 4.64 us -> none  [the longest x1 3.93 us: local(): jnp.dot(shared_hidden, shared_down, preferred_element_type=F32)]
  transfers between devices with their start and end apart: 10 -> 2, of which waited for: 3 -> 0; matrix products, arithmetic and copies ran while one was open for 1% -> 2% of each run, Pallas kernels for 17% -> 1%
where the time goes in v2:
time: 290 us
  Pallas kernels  271 us (93%)
  local copies, waits for them, and re-layouts  14.5 us (5%)
  starting transfers between devices  3.57 us (1%)
    pallas_call x1, Pallas kernels, experts(): pl.pallas_call(moe_kernel, name='experts', in_specs=[VM] * 6 + [ANY] * 7,...  199 us
    pallas_call x1, Pallas kernels, scan_states(): pl.pallas_call(scan_kernel, name='scan_states', in_specs=[VM, ANY], out_s...  56.4 us
    unnamed x29, local copies, waits for them, and re-layouts  12.3 us
    pallas_call x1, Pallas kernels, local_terms(): pl.pallas_call(local_kernel, name='local_terms', grid=(steps,), in_specs=...  9.39 us
  transfers between devices with their start and end apart: 2, of which 0 were waited for; matrix products, arithmetic and copies ran while one was open for 2% of the time, Pallas kernels for 1%

profile of v2, /device:TPU:51, one launch (start us, length us, event | category | flops | bytes accessed | tf_op | source)
XLA Modules:
  0.0 289.7 jit_solution(7272146046093047847)
XLA Ops:
  0.0 0.7 collective-permute-start.1
  0.7 0.8 slice.3
  1.5 2.9 %collective-permute-start = (bf16[8,4096]{1,0:T(8,128)(2,1)S(1)}, bf16[8,4096]{1,0:T(8,128)(2,1)S(1)}, u32[]{:S(2)}, u32[]{:S(2)}) collective-permute-start(bf16[8,4096]{1,0:T(8,128)(2,1)S(1)} %slice.3), channel_id=1, source_target_pairs={{0,1},{1,2},{2,3},{3,4},{4,5},{5,6},{6,7},{7,8},{8,9},{9,10},{10,1... | collective-permute-start | bytes 196616 | tf_op jit(solution)/shard_map/ppermute | solution.py:692
  4.4 0.8 copy.25.ld_ref
  5.2 0.8 copy.26.ws_ref
  6.0 1.3 reshape.19.switch
  7.3 0.0 collective-permute-done.1
  7.3 0.7 pad_add_fusion
  8.0 0.1 copy.24.ids_ref
  8.1 0.0 copy-start.6
  8.1 0.8 copy-done.6
  8.9 0.0 copy-start.5
  8.9 2.3 slots.1.sel
  11.2 0.0 copy-start.2
  11.2 1.0 copy-done.2
  12.2 0.0 copy-start.1
  12.2 0.0 collective-permute-done.qb_ref.kb_ref.vb_ref
  12.2 0.0 copy-start.8
  12.2 1.4 copy-done.8
  13.6 0.0 copy-start.12
  13.6 0.8 copy-done.12
  14.4 9.4 %local_terms.1 = (bf16[16,256,128]{2,1,0:T(8,128)(2,1)S(1)}, bf16[16,128,128]{2,1,0:T(8,128)(2,1)S(1)}, f32[16,128,128]{2,1,0:T(8,128)S(1)}) custom-call(bf16[128,4096]{1,0:T(8,128)(2,1)S(1)} %copy-done.8, bf16[128,4096]{1,0:T(8,128)(2,1)S(1)} %copy-done.8, bf16[128,4096]{1,0:T(8,128)(2,1)S(1)} %copy-done.8, ...), custom_call_target="tpu_custom_call" | custom-call | flops 8000000000 | bytes 6000000 | tf_op jit(solution)/shard_map/local_terms/pallas_call | solution.py:146
  23.8 0.0 copy-done.5
  23.8 0.0 copy-done.1
  23.8 0.0 copy-start.3
  23.8 0.0 copy-start.4
  23.8 0.0 copy-start.7
  23.9 0.0 copy-start.9
  23.9 56.4 %scan_states.1 = (bf16[16,128,128]{2,1,0:T(8,128)(2,1)S(1)}, bf16[4,2,4,2,128,512]{5,4,3,2,1,0:T(8,128)(2,1)S(1)}) custom-call(bf16[16,256,128]{2,1,0:T(8,128)(2,1)S(1)} %get-tuple-element.17.maps, bf16[2,4,2,128,512]{4,3,2,1,0:T(8,128)(2,1)S(1)} %bitcast.5), custom_call_target="tpu_custom_call" | custom-call | flops 30000001024 | bytes 4000000 | tf_op jit(solution)/shard_map/scan_states/pallas_call | solution.py:335
  80.2 0.0 copy-start
  80.3 3.2 %copy-done = bf16[4,2,4,2,128,512]{5,4,3,2,1,0:T(8,128)(2,1)} copy-done((bf16[4,2,4,2,128,512]{5,4,3,2,1,0:T(8,128)(2,1)}, bf16[4,2,4,2,128,512]{5,4,3,2,1,0:T(8,128)(2,1)S(1)}, u32[]{:S(2)}) %copy-start) | copy-done | bytes 8388632
  83.5 0.0 copy-done.3
  83.5 0.0 copy-done.4
  83.5 0.0 copy-done.7
  83.5 0.0 copy-done.9
  83.5 4.0 %mix.1 = (bf16[128,2048]{1,0:T(8,128)(2,1)S(1)}, bf16[128,2048]{1,0:T(8,128)(2,1)S(1)}) custom-call(bf16[16,128,128]{2,1,0:T(8,128)(2,1)S(1)} %get-tuple-element.15.reads, f32[16,128,128]{2,1,0:T(8,128)S(1)} %get-tuple-element.16.offs, bf16[16,128,128]{2,1,0:T(8,128)(2,1)S(1)} %get-tuple-element.18.starts, bf16[128,2048]{1,0:T(8,128)(2,1)S(1)} %copy-done.3, ...), custom_call_target="tpu_custom_call" | custom-call | flops 2000000000 | bytes 12000000 | tf_op jit(solution)/shard_map/mix/pallas_call | solution.py:405
  87.5 0.0 copy-start.10
  87.5 0.8 copy-done.10
  88.3 0.0 copy-start.11
  88.3 0.8 copy-done.11
  89.1 198.7 %experts.1 = bf16[128,2048]{1,0:T(8,128)(2,1)} custom-call(bf16[128,2048]{1,0:T(8,128)(2,1)} %copy-done.11, bf16[128,2048]{1,0:T(8,128)(2,1)} %copy-done.10, bf16[256,1536]{1,0:T(8,128)(2,1)} %copy-done.2, s32[256,10]{1,0:T(8,128)} %copy-done.5, s32[8,1536]{1,0:T(8,128)} %constant.2.clone.table_ref, bf16[1,2048]{1,0:T(2,128)(2,1)} %reshape.19.switch, ...), custom_call_target="tpu_custom_call" | custom-call | flops 60000002048 | bytes 30000000 | tf_op jit(solution)/shard_map/experts/pallas_call | solution.py:655
  287.8 1.9 copy.29
Async XLA Ops:
  0.0 7.3 %collective-permute-start.1 = (s32[128,10]{0,1:T(8,128)}, s32[128,10]{0,1:T(8,128)S(1)}, u32[]{:S(2)}, u32[]{:S(2)}) collective-permute-start(s32[128,10]{0,1:T(8,128)} %param.29), channel_id=1, source_target_pairs={{0,4},{4,0},{1,5},{5,1},{2,6},{6,2},{3,7},{7,3},{8,12},{12,8},{9,1... | collective-permute-start | bytes 15368 | tf_op jit(solution)/shard_map/ppermute | solution.py:683
  1.5 10.7 %collective-permute-start = (bf16[8,4096]{1,0:T(8,128)(2,1)S(1)}, bf16[8,4096]{1,0:T(8,128)(2,1)S(1)}, u32[]{:S(2)}, u32[]{:S(2)}) collective-permute-start(bf16[8,4096]{1,0:T(8,128)(2,1)S(1)} %slice.3), channel_id=1, source_target_pairs={{0,1},{1,2},{2,3},{3,4},{4,5},{5,6},{6,7},{7,8},{8,9},{9,10},{10,1... | collective-permute-start | bytes 196616 | tf_op jit(solution)/shard_map/ppermute | solution.py:692
  8.1 0.8 copy-start.6
  8.9 14.9 %copy-start.5 = (s32[256,10]{1,0:T(8,128)}, s32[256,10]{1,0:T(8,128)S(1)}, u32[]{:S(2)}) copy-start(s32[256,10]{1,0:T(8,128)S(1)} %copy.24.ids_ref) | copy-start | bytes 30724
  11.2 1.0 copy-start.2
  12.2 11.6 %copy-start.1 = (bf16[2048,512]{1,0:T(8,128)(2,1)S(1)}, bf16[2048,512]{1,0:T(8,128)(2,1)}, u32[]{:S(2)}) copy-start(bf16[2048,512]{1,0:T(8,128)(2,1)} %own.1) | copy-start | bytes 6291460
  12.2 1.4 copy-start.8
  13.6 0.8 copy-start.12
  23.8 59.6 %copy-start.3 = (bf16[128,2048]{1,0:T(8,128)(2,1)S(1)}, bf16[128,2048]{1,0:T(8,128)(2,1)}, u32[]{:S(2)}) copy-start(bf16[128,2048]{1,0:T(8,128)(2,1)} %gate_ref.1) | copy-start | bytes 1572868
  23.8 59.6 %copy-start.4 = (bf16[128,2048]{1,0:T(8,128)(2,1)S(1)}, bf16[128,2048]{1,0:T(8,128)(2,1)}, u32[]{:S(2)}) copy-start(bf16[128,2048]{1,0:T(8,128)(2,1)} %res_ref.1) | copy-start | bytes 1572868
  23.8 59.6 %copy-start.7 = (f32[2048]{0:T(1024)S(1)}, f32[2048]{0:T(1024)}, u32[]{:S(2)}) copy-start(f32[2048]{0:T(1024)} %param.27) | copy-start | bytes 24580
  23.9 59.6 %copy-start.9 = (f32[128]{0:T(128)S(1)}, f32[128]{0:T(128)}, u32[]{:S(2)}) copy-start(f32[128]{0:T(128)} %param.25) | copy-start | bytes 1540
  80.2 3.2 %copy-start = (bf16[4,2,4,2,128,512]{5,4,3,2,1,0:T(8,128)(2,1)}, bf16[4,2,4,2,128,512]{5,4,3,2,1,0:T(8,128)(2,1)S(1)}, u32[]{:S(2)}) copy-start(bf16[4,2,4,2,128,512]{5,4,3,2,1,0:T(8,128)(2,1)S(1)} %get-tuple-element.19) | copy-start | bytes 25165828
  87.5 0.8 copy-start.10
  88.3 0.8 copy-start.11

commit v3 on v2

v3 whole, which is shorter than its diff:
```python
import jax
import jax.numpy as jnp
import numpy as np
from jax import lax
from jax.experimental import pallas as pl
from jax.experimental.pallas import tpu as pltpu
from jax.sharding import Mesh
from jax.sharding import PartitionSpec as P

VHEADS = 16
HEAD = 128
ROWS = 128
TOP = 10
CAP = 6
WIDTH = 2048
EXPERTS = 256
AXES = ("ctx_0", "ctx_1", "ctx_2", "exp")
PEERS = 64
SLOTS = 4 * CAP
SENT = PEERS * SLOTS
BATCH = 8
MESH = pl.DeviceIdType.MESH
epsilon = 1e-06
F32 = jnp.float32
BF16 = jnp.bfloat16
VM = pl.BlockSpec(memory_space=pltpu.VMEM)
ANY = pl.BlockSpec(memory_space=pl.ANY)


def nn(a, b):
    return lax.dot_general(a, b, (((1,), (0,)), ((), ())), preferred_element_type=F32)


def nt(a, b):
    return lax.dot_general(a, b, (((1,), (1,)), ((), ())), preferred_element_type=F32)


def tn(a, b):
    return lax.dot_general(a, b, (((0,), (0,)), ((), ())), preferred_element_type=F32)


def silu(v):
    return v / (1.0 + jnp.exp(-v))


def front_kernel(
    mixed, conv, decay_ref, strength_ref, ids_ref, table_ref, gate_ref, gain_ref, res_ref,
    post_ref, weight,
    after_ref, routed_ref, sel_ref, all_ids,
    there, tail, ids_there, pad, cumt, lows, inv, maps, reads, offs, wall, normed, mixed_rows,
    got1, pre1, tot1, got2, pre2, tot2, got3, st4, got4, st5, got5,
    own_sem, send0, recv0, send1, recv1, send2, recv2, send3, recv3, send4, recv4, send5, recv5,
    sendw1, recvw1, sendw2, recvw2, sendw3, recvw3,
):
    z, x, c, y = (lax.axis_index(a) for a in AXES)
    place = 2 * x + c
    spot = (z * 4 + x) * 8 + c * 4 + y
    partner = {"ctx_2": 1 - c}
    barrier = pltpu.get_barrier_semaphore()

    def whole(k):
        return {
            "ctx_0": k // 32, "ctx_1": lax.rem(k // 8, 4), "ctx_2": lax.rem(k // 4, 2),
            "exp": lax.rem(k, 4),
        }

    following, previous = whole(lax.rem(spot + 1, 128)), whole(lax.rem(spot + 127, 128))

    def at(j, axis):
        if axis == "y":
            return {"exp": lax.rem(y + j, 4)}
        if axis == "z":
            return {"ctx_0": lax.rem(z + j, 4)}
        if axis == "x":
            return {"ctx_1": lax.rem(x + j, 4)}
        other = lax.rem(place + j, 8)
        return {"ctx_1": other // 2, "ctx_2": lax.rem(other, 2)}

    for device in (following, previous):
        pl.semaphore_signal(barrier, inc=1, device_id=device, device_id_type=MESH)
    for axis, count in (("y", 4), ("z", 4), ("p", 8)):
        for j in range(1, count):
            pl.semaphore_signal(barrier, inc=1, device_id=at(j, axis), device_id_type=MESH)
    own = pltpu.make_async_copy(weight, wall.at[y], own_sem)
    own.start()
    pl.semaphore_wait(barrier, 15)
    started = []

    def remote(src, dst, s, r, device):
        return pltpu.make_async_remote_copy(
            src_ref=src, dst_ref=dst, send_sem=s, recv_sem=r, device_id=device, device_id_type=MESH
        )

    def send(*args):
        copy = remote(*args)
        copy.start()
        started.append(copy)
        return copy

    last_rows = send(mixed.at[ROWS - 16 : ROWS], tail, send0.at[0], recv0.at[0], following)
    ids_copy = send(ids_ref, ids_there, send0.at[1], recv0.at[1], partner)
    first = []
    for j in range(1, 4):
        for part, quarter in ((0, x), (1, z)):
            first.append(
                send(
                    weight.at[part, quarter, c], wall.at[y, part, quarter, c],
                    sendw1.at[j, part], recvw1.at[j, part], at(j, "y"),
                )
            )

    rows = lax.broadcasted_iota(jnp.int32, (ROWS, ROWS), 0)
    cols = lax.broadcasted_iota(jnp.int32, (ROWS, ROWS), 1)
    causal = rows >= cols
    strict = rows > cols
    ones = causal.astype(F32)
    eye = (rows == cols).astype(F32)
    eye_b = eye.astype(BF16)

    earlier = strict.astype(BF16)
    wanted = wanted_experts(table_ref)
    source, slot = table_ref[4:5, :], table_ref[5:6, :]
    ids_copy.wait_recv()
    for half, held in ((0, ids_ref), (1, ids_there)):
        ids = nt(eye_b, held[...].astype(F32).astype(BF16))
        all_ids[half * ROWS : (half + 1) * ROWS, :] = ids
        aim = jnp.where(source == half, wanted, -1).astype(F32)
        hit = ids[:, 0:1] == aim
        for k in range(1, TOP):
            hit = hit | (ids[:, k : k + 1] == aim)
        marks = hit.astype(F32)
        rank = nn(earlier, marks.astype(BF16))
        sel_ref[half * ROWS : (half + 1) * ROWS, :] = jnp.where(
            rank == slot.astype(F32), marks, 0.0
        ).astype(BF16)

    decay, highest = decay_ref[...], lax.Precision.HIGHEST

    def exact(p, q):
        return lax.dot_general(
            p, q, (((1,), (1,)), ((), ())), precision=highest, preferred_element_type=F32
        )

    cum = exact(ones, decay)
    cumt[...] = exact(decay, ones)
    strength = exact(eye, strength_ref[...])
    lane = lax.broadcasted_iota(jnp.int32, (ROWS, VHEADS), 1)

    def column(table, head):
        return jnp.sum(jnp.where(lane == head, table, 0.0), axis=1, keepdims=True)

    def activated(begin, n):
        here = pl.ds(pl.multiple_of(begin, HEAD), n)
        pad[0:8, 0:n] = jnp.where(spot > 0, tail[8:16, here].astype(F32), 0.0)
        pad[8 : 8 + ROWS, 0:n] = mixed[:, here].astype(F32)
        total = conv[3:4, here] * pad[8 : 8 + ROWS, 0:n]
        for tap in range(3):
            total = total + conv[tap : tap + 1, here] * pad[5 + tap : 5 + tap + ROWS, 0:n]
        return silu(total)

    def unit(a):
        return a * lax.rsqrt(jnp.sum(a * a, axis=-1, keepdims=True) + epsilon)

    last_rows.wait_recv()

    def terms(batch, _):
        groups = [lax.rem(y + 1 + 2 * batch + part, 4) for part in range(2)]
        heads = [4 * groups[i // 4] + i % 4 for i in range(BATCH)]
        n = 2 * HEAD
        queries = [activated(g * n, n) for g in groups]
        keys = [activated(WIDTH // 2 + g * n, n) for g in groups]
        values = [activated(WIDTH + 2 * g * n, 2 * n) for g in groups]
        per_head = []
        for pair in range(BATCH // 2):
            part = slice(pair % 2 * HEAD, (pair % 2 + 1) * HEAD)
            query = unit(queries[pair // 2][:, part]) * HEAD ** (-0.5)
            key = unit(keys[pair // 2][:, part])
            key_b = key.astype(BF16)
            inner = nt(key_b, key_b)
            scores = nt(query.astype(BF16), key_b)
            for i in (2 * pair, 2 * pair + 1):
                d = column(cum, heads[i])
                b = column(strength, heads[i])
                gap = d - cumt[pl.ds(heads[i], 1), :]
                ratios = jnp.where(causal, jnp.exp(jnp.where(causal, gap, 0.0)), 0.0)
                low = jnp.where(strict, ratios * inner, 0.0) * b
                lows[i] = low
                inv[i] = eye - jnp.where((rows >> 1) == (cols >> 1), low, 0.0)
                end = d[ROWS - 1 : ROWS, :]
                decays = jnp.exp(d)
                right = jnp.concatenate(
                    [
                        (b * decays * key).astype(BF16),
                        (b * values[i // 4][:, i % 4 * HEAD : (i % 4 + 1) * HEAD]).astype(BF16),
                    ],
                    axis=1,
                )
                per_head.append(
                    (
                        (scores * ratios).astype(BF16),
                        query * decays,
                        (key * jnp.exp(end - d)).astype(BF16),
                        right,
                        jnp.exp(end) - 1.0,
                    )
                )
        for level in range(1, 7):
            here = (rows >> (level + 1)) == (cols >> (level + 1))
            here = here & ((rows >> level) != (cols >> level))
            for i in range(BATCH):
                now = inv[i]
                now_b = now.astype(BF16)
                off = jnp.where(here, lows[i], 0.0).astype(BF16)
                inv[i] = now - nn(now_b, nn(off, now_b).astype(BF16))
        for i in range(BATCH):
            score, read, end_key, right, less = per_head[i]
            solved = nn(inv[i].astype(BF16), right).astype(BF16)
            carried = tn(solved, end_key)
            maps[heads[i], 0:HEAD, :] = (less * eye - carried[0:HEAD]).astype(BF16)
            maps[heads[i], HEAD : 2 * HEAD, :] = carried[HEAD:].astype(BF16)
            produced = nn(score, solved)
            reads[heads[i]] = (read - produced[:, 0:HEAD]).astype(BF16)
            offs[heads[i]] = produced[:, HEAD:]
        for other in groups:
            four = maps.at[pl.ds(4 * other, 4)]

            @pl.when(other != y)
            def _():
                remote(four, got1.at[y], send1.at[other], recv1.at[y], {"exp": other}).start()

            @pl.when(other == y)
            def _():
                pltpu.make_async_copy(four, got1.at[y], recv1.at[y]).start()

        return 0

    lax.fori_loop(0, VHEADS // BATCH, terms, 0)

    for copy in first:
        copy.wait_recv()

    def spread(k):
        copies = []
        for j in range(1, 4):
            other = lax.rem(y + j, 4)
            for part, quarter, device in ((0, x, at(k, "x")), (1, z, at(k, "z"))):
                held = wall.at[other, part, quarter, c]
                copies.append(
                    send(held, held, sendw2.at[k, j, part], recvw2.at[k, j, part], device)
                )
        return copies

    def across(k):
        copies = []
        for j in range(1, 4):
            other = lax.rem(y + j, 4)
            for part, quarter in ((0, lax.rem(x + 4 - k, 4)), (1, lax.rem(z + 4 - k, 4))):
                held = wall.at[other, part, quarter, c]
                copies.append(
                    send(held, held, sendw3.at[k, j, part], recvw3.at[k, j, part], partner)
                )
        return copies

    second = spread(1) + spread(3)
    third = across(0)

    for m in range(4):
        pltpu.make_async_copy(got1.at[m], got1.at[m], recv1.at[m]).wait()
    for h in range(4):
        run = got1[0, h].astype(F32)
        for m in range(1, 4):
            pre1[m - 1, h] = run.astype(BF16)
            run = run + got1[m, h].astype(F32) + nn(run.astype(BF16), got1[m, h, 0:HEAD, :])
        tot1[h] = run.astype(BF16)

    copies = []
    for j in range(1, 8):
        other = lax.rem(place + j, 8)
        head, half = other // 2, lax.rem(other, 2)
        copies.append(
            send(
                tot1.at[head, 0:HEAD], got2.at[place, 0:HEAD], send2.at[j, 0], recv2.at[j, 0],
                at(j, "p"),
            )
        )
        copies.append(
            send(
                tot1.at[head, pl.ds(pl.multiple_of(HEAD + 64 * half, 64), 64)],
                got2.at[place, HEAD : HEAD + 64],
                send2.at[j, 1], recv2.at[j, 1], at(j, "p"),
            )
        )
    got2[place, 0:HEAD, :] = tot1[x, 0:HEAD, :]
    got2[place, HEAD : HEAD + 64, :] = tot1[x, pl.ds(pl.multiple_of(HEAD + 64 * c, 64), 64), :]
    for copy in copies:
        copy.wait_recv()
    run = got2[0].astype(F32)
    for p in range(1, 8):
        pre2[p - 1] = run.astype(BF16)
        run = run + got2[p].astype(F32) + nn(run.astype(BF16), got2[p, 0:HEAD, :])
    tot2[...] = run.astype(BF16)

    copies = []
    for j in range(1, 4):
        copies.append(send(tot2, got3.at[z], send3.at[j], recv3.at[j], at(j, "z")))
    got3[z] = tot2[...]
    for copy in copies:
        copy.wait_recv()
    state = jnp.zeros((64, HEAD), F32)
    for k in range(3):
        later = state + got3[k, HEAD:, :].astype(F32) + nn(state.astype(BF16), got3[k, 0:HEAD, :])
        state = jnp.where(k < z, later, state)
    state_b = state.astype(BF16)
    st4[0] = state_b
    for p in range(1, 8):
        st4[p] = (
            state + pre2[p - 1, HEAD:, :].astype(F32) + nn(state_b, pre2[p - 1, 0:HEAD, :])
        ).astype(BF16)

    copies = []
    rows_here = pl.ds(pl.multiple_of(64 * c, 64), 64)
    for j in range(1, 8):
        other = lax.rem(place + j, 8)
        copies.append(
            send(st4.at[other], got4.at[x, rows_here], send4.at[j], recv4.at[j], at(j, "p"))
        )
    got4[x, rows_here, :] = st4[place]
    second_last = spread(2)
    for copy in second:
        copy.wait_recv()
    third += across(1) + across(3)
    for copy in copies:
        copy.wait_recv()
    for h in range(4):
        begin = got4[h]
        st5[0, h] = begin
        for m in range(1, 4):
            st5[m, h] = (
                begin.astype(F32)
                + pre1[m - 1, h, HEAD:, :].astype(F32)
                + nn(begin, pre1[m - 1, h, 0:HEAD, :])
            ).astype(BF16)

    copies = []
    for j in range(1, 4):
        other = lax.rem(y + j, 4)
        copies.append(send(st5.at[other], got5.at[y], send5.at[j], recv5.at[j], at(j, "y")))
    got5[y] = st5[y]
    for copy in second_last:
        copy.wait_recv()
    third += across(2)
    for copy in copies:
        copy.wait_recv()

    gain = gain_ref[...]
    for h in range(VHEADS):
        part = slice(h * HEAD, (h + 1) * HEAD)
        out = offs[h] + nt(reads[h], got5[h // 4, h % 4])
        out = out * lax.rsqrt(jnp.mean(out * out, axis=-1, keepdims=True) + epsilon)
        normed[:, part] = (out * gain * silu(gate_ref[:, part].astype(F32))).astype(BF16)
    own.wait()
    for copy in third:
        copy.wait_recv()
    columns = WIDTH // 4
    for k in range(4):
        here = slice(k * columns, (k + 1) * columns)
        mixed_rows[:, here] = nn(normed[...], wall[k].reshape(WIDTH, columns))
    after = (res_ref[...].astype(F32) + mixed_rows[...]).astype(BF16)
    after_ref[...] = after
    wide = after.astype(F32)
    normed[...] = (
        wide * lax.rsqrt(jnp.mean(wide * wide, axis=-1, keepdims=True) + epsilon) * post_ref[...]
    ).astype(BF16)
    rows_copy = send(normed, there, send0.at[2], recv0.at[2], partner)
    routed_ref[0:ROWS, :] = normed[...]
    rows_copy.wait_recv()
    routed_ref[ROWS : 2 * ROWS, :] = there[...]
    for copy in started:
        copy.wait_send()
    for other in range(4):

        @pl.when(other != y)
        def _():
            pltpu.make_async_copy(got1.at[other], got1.at[other], send1.at[other]).wait()


def front(mixed, conv_weight, decay, strength, ids, gate, gain, residual, post, out_weight):
    dma = pltpu.SemaphoreType.DMA
    cut = (2, 4, 2, WIDTH // 16, WIDTH // 4)
    shape = jax.ShapeDtypeStruct((ROWS, WIDTH), BF16)
    return pl.pallas_call(
        front_kernel,
        name="front",
        in_specs=[VM] * 10 + [ANY],
        out_specs=[VM] * 4,
        out_shape=[
            shape, jax.ShapeDtypeStruct((2 * ROWS, WIDTH), BF16),
            jax.ShapeDtypeStruct((2 * ROWS, SENT), BF16),
            jax.ShapeDtypeStruct((2 * ROWS, TOP), F32),
        ],
        scratch_shapes=[
            pltpu.VMEM((ROWS, WIDTH), BF16),
            pltpu.VMEM((16, 2 * WIDTH), BF16),
            pltpu.VMEM((TOP, ROWS), jnp.int32),
            pltpu.VMEM((8 + ROWS, 4 * HEAD), F32),
            pltpu.VMEM((VHEADS, ROWS), F32),
            pltpu.VMEM((BATCH, ROWS, ROWS), F32),
            pltpu.VMEM((BATCH, ROWS, ROWS), F32),
            pltpu.VMEM((VHEADS, 2 * HEAD, HEAD), BF16),
            pltpu.VMEM((VHEADS, ROWS, HEAD), BF16),
            pltpu.VMEM((VHEADS, ROWS, HEAD), F32),
            pltpu.VMEM((4, *cut), BF16),
            pltpu.VMEM((ROWS, WIDTH), BF16),
            pltpu.VMEM((ROWS, WIDTH), F32),
            pltpu.VMEM((4, 4, 2 * HEAD, HEAD), BF16),
            pltpu.VMEM((3, 4, 2 * HEAD, HEAD), BF16),
            pltpu.VMEM((4, 2 * HEAD, HEAD), BF16),
            pltpu.VMEM((8, HEAD + 64, HEAD), BF16),
            pltpu.VMEM((7, HEAD + 64, HEAD), BF16),
            pltpu.VMEM((HEAD + 64, HEAD), BF16),
            pltpu.VMEM((4, HEAD + 64, HEAD), BF16),
            pltpu.VMEM((8, 64, HEAD), BF16),
            pltpu.VMEM((4, HEAD, HEAD), BF16),
            pltpu.VMEM((4, 4, HEAD, HEAD), BF16),
            pltpu.VMEM((4, 4, HEAD, HEAD), BF16),
            dma, dma((3,)), dma((3,)), dma((4,)), dma((4,)), dma((8, 2)), dma((8, 2)),
            dma((4,)), dma((4,)), dma((8,)), dma((8,)), dma((4,)), dma((4,)),
            dma((4, 2)), dma((4, 2)), dma((4, 4, 2)), dma((4, 4, 2)), dma((4, 4, 2)),
            dma((4, 4, 2)),
        ],
        compiler_params=pltpu.CompilerParams(
            collective_id=0, has_side_effects=True, vmem_limit_bytes=56 << 20
        ),
        cost_estimate=pl.CostEstimate(
            flops=30_000_000_000, bytes_accessed=14_000_000, transcendentals=1_500_000
        ),
    )(
        mixed, conv_weight, decay, strength, ids, jnp.asarray(TABLE), gate, gain, residual, post,
        out_weight.reshape(cut),
    )


def distance(group, i):
    dx = lax.rem(i, 4)
    dy = lax.rem(dx + lax.rem(group, 4), 4)
    dz = lax.rem(dx + 2 * (i // 4) + group // 4, 4)
    return dz, dx, dy


LANES = np.arange(SENT)
PEER, INSIDE = LANES // SLOTS, LANES % SLOTS
NEAR = PEER % 8
TABLE = np.stack(
    [
        (NEAR + 2 * (NEAR // 4) + PEER // 32) % 4,
        NEAR % 4,
        (NEAR + PEER // 8) % 4,
        INSIDE // (2 * CAP),
        INSIDE % (2 * CAP) // CAP,
        INSIDE % CAP,
        0 * LANES,
        0 * LANES,
    ]
).astype(np.int32)


def wanted_experts(table_ref, lanes=slice(None)):
    z, x, c, y = (lax.axis_index(a) for a in AXES)
    there = ((table_ref[0:1, lanes] + z) & 3) * 32 + ((table_ref[1:2, lanes] + x) & 3) * 8
    there = there + c * 4 + ((table_ref[2:3, lanes] + y) & 3)
    return 2 * there + table_ref[3:4, lanes]


GROUPS, EACH = 8, 8
BUILT = 2 * EACH * SLOTS


def moe_kernel(
    routed, after, sel, ids_ref, table_ref, switch, router, s_gate, s_up, s_down, gate, up, down,
    out_ref, out_buf, in_buf, back_buf, high, low, total, swap, theirs,
    v_router, v_sgate, v_sup, v_sdown, v_gate, v_up, v_down,
    load_sems, send1, recv1, send2, recv2, send_y, recv_y,
):
    z, x, c, y = (lax.axis_index(a) for a in AXES)
    partner = {"ctx_2": 1 - c}
    barrier = pltpu.get_barrier_semaphore()

    def peer(group, i, sign):
        dz, dx, dy = distance(group, i)
        return {
            "ctx_0": lax.rem(z + 4 + sign * dz, 4),
            "ctx_1": lax.rem(x + 4 + sign * dx, 4),
            "exp": lax.rem(y + 4 + sign * dy, 4),
        }

    def greet(k, _):
        pl.semaphore_signal(
            barrier, inc=1, device_id=peer(k // EACH, lax.rem(k, EACH), 1), device_id_type=MESH
        )
        return 0

    lax.fori_loop(1, PEERS, greet, 0)
    pl.semaphore_signal(barrier, inc=1, device_id=partner, device_id_type=MESH)
    loads = [
        pltpu.make_async_copy(src, dst, load_sems.at[k])
        for k, (src, dst) in enumerate(
            (
                (router, v_router), (s_gate, v_sgate), (s_up, v_sup), (s_down, v_sdown),
                (gate, v_gate), (up, v_up), (down, v_down),
            )
        )
    ]
    for load in loads:
        load.start()

    def build(p):
        lanes = slice(p * BUILT, (p + 1) * BUILT)
        built = tn(sel[:, lanes], routed[...]).astype(BF16)
        out_buf[2 * p * EACH : 2 * (p + 1) * EACH] = built.reshape(2 * EACH, SLOTS, WIDTH)

    build(0)
    pl.semaphore_wait(barrier, PEERS)

    def remote(src, dst, s, r, device):
        return pltpu.make_async_remote_copy(
            src_ref=src, dst_ref=dst, send_sem=s, recv_sem=r, device_id=device, device_id_type=MESH
        )

    def dispatch(group, begin):
        def one(i, _):
            g = group * EACH + i
            remote(
                out_buf.at[g], in_buf.at[g], send1.at[group], recv1.at[group], peer(group, i, 1)
            ).start()
            return 0

        lax.fori_loop(begin, EACH, one, 0)

    def give_back(group, begin):
        def one(i, _):
            g = group * EACH + i
            remote(
                in_buf.at[g], back_buf.at[g], send2.at[group], recv2.at[group], peer(group, i, -1)
            ).start()
            return 0

        lax.fori_loop(begin, EACH, one, 0)

    for p in range(GROUPS // 2):
        if p:
            build(p)
        dispatch(2 * p, 0 if p else 1)
        dispatch(2 * p + 1, 0)
        if p == 0:
            pltpu.make_async_copy(out_buf.at[0], in_buf.at[0], recv1.at[0]).start()

    loads[0].wait()
    logits = nn(routed[...], v_router[...])
    lane = lax.broadcasted_iota(jnp.int32, (2 * ROWS, EXPERTS), 1).astype(F32)
    ids = ids_ref[...]
    hit = ids[:, 0:1] == lane
    for k in range(1, TOP):
        hit = hit | (ids[:, k : k + 1] == lane)
    chosen = jnp.where(hit, jnp.exp(jnp.where(hit, logits, 0.0)), 0.0)
    gates = chosen / jnp.sum(chosen, axis=1, keepdims=True)
    gates_high = gates.astype(BF16)
    gates_low = (gates - gates_high.astype(F32)).astype(BF16)
    for p in range(GROUPS // 2):
        lanes = slice(p * BUILT, (p + 1) * BUILT)
        spread = (
            lax.broadcasted_iota(jnp.int32, (EXPERTS, BUILT), 0) == wanted_experts(table_ref, lanes)
        ).astype(BF16)
        high[p] = nn(gates_high, spread).astype(BF16) * sel[:, lanes]
        low[p] = nn(gates_low, spread).astype(BF16) * sel[:, lanes]

    for load in loads[1:4]:
        load.wait()
    mine = routed[0:ROWS, :]
    hidden = (silu(nn(mine, v_sgate[...])) * nn(mine, v_sup[...])).astype(BF16)
    open_ = jnp.sum(mine.astype(F32) * switch[...].astype(F32), axis=1, keepdims=True)
    total[0:ROWS, :] = after[...].astype(F32) + nn(hidden, v_sdown[...]) / (1.0 + jnp.exp(-open_))
    total[ROWS:, :] = jnp.zeros((ROWS, WIDTH), F32)

    for load in loads[4:]:
        load.wait()

    def serve(group, begin):
        here = pl.ds(group * EACH, EACH)
        pltpu.make_async_copy(in_buf.at[here], in_buf.at[here], recv1.at[group]).wait()
        n = EACH * SLOTS
        rows = in_buf[here].reshape(n, WIDTH)
        inside = lax.rem(lax.broadcasted_iota(jnp.int32, (n, 1), 0), SLOTS)
        result = None
        for e in range(2):
            hidden = silu(nn(rows, v_gate[e])) * nn(rows, v_up[e])
            hidden = jnp.where((inside >= 2 * CAP) == bool(e), hidden, 0.0).astype(BF16)
            part = nn(hidden, v_down[e])
            result = part if result is None else result + part
        in_buf[here] = result.astype(BF16).reshape(EACH, SLOTS, WIDTH)

    serve(0, 1)
    pltpu.make_async_copy(in_buf.at[0], back_buf.at[0], recv2.at[0]).start()
    give_back(0, 1)

    def later(group, _):
        serve(group, 0)
        give_back(group, 0)
        return 0

    lax.fori_loop(1, GROUPS, later, 0)

    for p in range(GROUPS // 2):
        for group in (2 * p, 2 * p + 1):
            here = pl.ds(group * EACH, EACH)
            pltpu.make_async_copy(back_buf.at[here], back_buf.at[here], recv2.at[group]).wait()
        rows = back_buf[2 * p * EACH : 2 * (p + 1) * EACH].reshape(BUILT, WIDTH)
        part = total[ROWS:, :] + nn(high[p, ROWS:, :], rows) + nn(low[p, ROWS:, :], rows)
        if p < GROUPS // 2 - 1:
            total[ROWS:, :] = part
        else:
            theirs[...] = part.astype(BF16)
            last = remote(theirs, swap, send_y, recv_y, partner)
            last.start()
        total[0:ROWS, :] += nn(high[p, 0:ROWS, :], rows) + nn(low[p, 0:ROWS, :], rows)

    last.wait_recv()
    out_ref[...] = (total[0:ROWS, :] + swap[...].astype(F32)).astype(BF16)

    last.wait_send()
    for group in range(GROUPS):
        here = pl.ds(1, EACH - 1) if group == 0 else pl.ds(group * EACH, EACH)
        pltpu.make_async_copy(out_buf.at[here], out_buf.at[here], send1.at[group]).wait()
        pltpu.make_async_copy(in_buf.at[here], in_buf.at[here], send2.at[group]).wait()


def experts(
    routed, after, sel, ids, switch, router, s_gate, s_up, s_down, gate, up, down
):
    dma = pltpu.SemaphoreType.DMA
    vmem = lambda a: pltpu.VMEM(a.shape, a.dtype)
    slabs = pltpu.VMEM((PEERS, SLOTS, WIDTH), BF16)
    weights = (router, s_gate, s_up, s_down, gate, up, down)
    return pl.pallas_call(
        moe_kernel,
        name="experts",
        in_specs=[VM] * 6 + [ANY] * 7,
        out_specs=VM,
        out_shape=jax.ShapeDtypeStruct((ROWS, WIDTH), BF16),
        scratch_shapes=[
            slabs, slabs, slabs,
            pltpu.VMEM((GROUPS // 2, 2 * ROWS, BUILT), BF16),
            pltpu.VMEM((GROUPS // 2, 2 * ROWS, BUILT), BF16),
            pltpu.VMEM((2 * ROWS, WIDTH), F32),
            pltpu.VMEM((ROWS, WIDTH), BF16),
            pltpu.VMEM((ROWS, WIDTH), BF16),
            *(vmem(w) for w in weights),
            dma((7,)), dma((GROUPS,)), dma((GROUPS,)), dma((GROUPS,)), dma((GROUPS,)),
            dma, dma,
        ],
        compiler_params=pltpu.CompilerParams(
            collective_id=1, has_side_effects=True, vmem_limit_bytes=62 << 20
        ),
        cost_estimate=pl.CostEstimate(
            flops=60_000_000_000, bytes_accessed=30_000_000, transcendentals=2_000_000
        ),
    )(routed, after, sel, ids, jnp.asarray(TABLE), switch, *weights)


def local(
    residual, mixed_qkv, output_gate, log_decay, write_strength, conv_weight, norm_gain,
    out_weight, post_gain, router_weight, expert_ids, expert_gate, expert_up, expert_down,
    shared_gate, shared_up, shared_down, shared_switch,
):
    after_mix, routed_in, sel, ids = front(
        mixed_qkv, conv_weight, log_decay.T, write_strength.T, expert_ids.T, output_gate,
        norm_gain.reshape(1, HEAD), residual, post_gain.reshape(1, WIDTH), out_weight,
    )
    return experts(
        routed_in, after_mix, sel, ids, shared_switch.reshape(1, WIDTH), router_weight,
        shared_gate, shared_up, shared_down, expert_gate, expert_up, expert_down,
    )


def solution(mesh):
    finer = Mesh(mesh.devices.reshape(4, 4, 2, mesh.shape["exp"]), AXES)
    rows = P(AXES, None)
    held = P(AXES, None, None)
    placed = (
        rows, rows, rows, rows, rows, P(), P(), P(None, "exp"), P(), P(), rows, held, held, held,
        P(), P(), P(), P(),
    )
    return jax.shard_map(local, mesh=finer, in_specs=placed, out_specs=rows, check_vma=False)
```

time: 290 us -> 271 us (0.934)
  the two profiles are of different devices: /device:TPU:51 before, /device:TPU:11 now
where the time goes in v3:
time: 271 us
  Pallas kernels  268 us (99%)
  local copies, waits for them, and re-layouts  3.17 us (1%)
    pallas_call x1, Pallas kernels, experts(): pl.pallas_call(moe_kernel, name='experts', in_specs=[VM] * 6 + [ANY] * 7,...  201 us
    pallas_call x1, Pallas kernels, front(): pl.pallas_call(front_kernel, name='front', in_specs=[VM] * 10 + [ANY], ou...  67 us

profile of v3, /device:TPU:11, one launch (start us, length us, event | category | flops | bytes accessed | tf_op | source)
XLA Modules:
  0.0 270.8 jit_solution(2655861138137284316)
XLA Ops:
  0.0 1.3 reshape.15.switch
  1.3 67.0 %front.1 = (bf16[128,2048]{1,0:T(8,128)(2,1)}, bf16[256,2048]{1,0:T(8,128)(2,1)}, bf16[256,1536]{1,0:T(8,128)(2,1)}, f32[256,10]{1,0:T(8,128)}) custom-call(bf16[128,4096]{1,0:T(8,128)(2,1)} %mixed.1, f32[4,4096]{1,0:T(4,128)} %conv.1, f32[16,128]{1,0:T(8,128)} %bitcast.7, f32[16,128]{1,0:T(8,128)} %bitcast.8, s32[10,128]{1,0:T(8,128)} %bitcast.9, ...), custom_call_target="tpu_custom_call" | custom-call | flops 30000001024 | bytes 14000000 | tf_op jit(solution)/shard_map/front/pallas_call | solution.py:391
  68.3 200.6 %experts.1 = bf16[128,2048]{1,0:T(8,128)(2,1)} custom-call(bf16[256,2048]{1,0:T(8,128)(2,1)} %get-tuple-element.9.routed, bf16[128,2048]{1,0:T(8,128)(2,1)} %get-tuple-element.10.after, bf16[256,1536]{1,0:T(8,128)(2,1)} %get-tuple-element.11.sel, f32[256,10]{1,0:T(8,128)} %get-tuple-element.12.ids_ref, s32[8,1536]{1,0:T(8,128)} %constant.2.clone.table_ref, ...), custom_call_target="tpu_custom_call" | custom-call | flops 60000002048 | bytes 30000000 | tf_op jit(solution)/shard_map/experts/pallas_call | solution.py:643
  268.9 1.9 copy.21

commit v4 on v3

--- a/solution.py
+++ b/solution.py
@@ -290,6 +290,7 @@
                 send2.at[j, 1], recv2.at[j, 1], at(j, "p"),
             )
         )
+    second_last = spread(2)
     got2[place, 0:HEAD, :] = tot1[x, 0:HEAD, :]
     got2[place, HEAD : HEAD + 64, :] = tot1[x, pl.ds(pl.multiple_of(HEAD + 64 * c, 64), 64), :]
     for copy in copies:
@@ -304,6 +305,9 @@
     for j in range(1, 4):
         copies.append(send(tot2, got3.at[z], send3.at[j], recv3.at[j], at(j, "z")))
     got3[z] = tot2[...]
+    for copy in second:
+        copy.wait_recv()
+    third += across(1) + across(3)
     for copy in copies:
         copy.wait_recv()
     state = jnp.zeros((64, HEAD), F32)
@@ -325,10 +329,9 @@
             send(st4.at[other], got4.at[x, rows_here], send4.at[j], recv4.at[j], at(j, "p"))
         )
     got4[x, rows_here, :] = st4[place]
-    second_last = spread(2)
-    for copy in second:
+    for copy in second_last:
         copy.wait_recv()
-    third += across(1) + across(3)
+    third += across(2)
     for copy in copies:
         copy.wait_recv()
     for h in range(4):
@@ -346,25 +349,29 @@
         other = lax.rem(y + j, 4)
         copies.append(send(st5.at[other], got5.at[y], send5.at[j], recv5.at[j], at(j, "y")))
     got5[y] = st5[y]
-    for copy in second_last:
-        copy.wait_recv()
-    third += across(2)
-    for copy in copies:
-        copy.wait_recv()
-
-    gain = gain_ref[...]
-    for h in range(VHEADS):
-        part = slice(h * HEAD, (h + 1) * HEAD)
-        out = offs[h] + nt(reads[h], got5[h // 4, h % 4])
-        out = out * lax.rsqrt(jnp.mean(out * out, axis=-1, keepdims=True) + epsilon)
-        normed[:, part] = (out * gain * silu(gate_ref[:, part].astype(F32))).astype(BF16)
     own.wait()
     for copy in third:
         copy.wait_recv()
+
+    gain = gain_ref[...]
     columns = WIDTH // 4
-    for k in range(4):
-        here = slice(k * columns, (k + 1) * columns)
-        mixed_rows[:, here] = nn(normed[...], wall[k].reshape(WIDTH, columns))
+    for j in (0, 1, 3, 2):
+        member = lax.rem(y + 4 - j, 4)
+        if j:
+            copies[j - 1].wait_recv()
+        four = []
+        for i in range(4):
+            h = 4 * member + i
+            gate_here = gate_ref[:, pl.ds(pl.multiple_of(HEAD * h, HEAD), HEAD)].astype(F32)
+            out = offs[h] + nt(reads[h], got5[member, i])
+            out = out * lax.rsqrt(jnp.mean(out * out, axis=-1, keepdims=True) + epsilon)
+            four.append((out * gain * silu(gate_here)).astype(BF16))
+        four = jnp.concatenate(four, axis=1)
+        for k in range(4):
+            here = slice(k * columns, (k + 1) * columns)
+            block = wall[k, member // 2, pl.ds(2 * lax.rem(member, 2), 2)]
+            added = nn(four, block.reshape(4 * HEAD, columns))
+            mixed_rows[:, here] = mixed_rows[:, here] + added if j else added
     after = (res_ref[...].astype(F32) + mixed_rows[...]).astype(BF16)
     after_ref[...] = after
     wide = after.astype(F32)
@@ -676,7 +683,7 @@
         norm_gain.reshape(1, HEAD), residual, post_gain.reshape(1, WIDTH), out_weight,
     )
     return experts(
-        routed_in, after_mix, sel, ids, shared_switch.reshape(1, WIDTH), router_weight,
+        routed_in, after_mix, sel, ids, shared_switch, router_weight,
         shared_gate, shared_up, shared_down, expert_gate, expert_up, expert_down,
     )
 

time: 271 us -> 264 us (0.974)
  the two profiles are of different devices: /device:TPU:11 before, /device:TPU:51 now
where the time goes in v4:
time: 264 us; the launch traced here: 258 us
  Pallas kernels  257 us (97%)
    pallas_call x1, Pallas kernels, experts(): pl.pallas_call(moe_kernel, name='experts', in_specs=[VM] * 6 + [ANY] * 7,...  186 us
    pallas_call x1, Pallas kernels, front(): pl.pallas_call(front_kernel, name='front', in_specs=[VM] * 10 + [ANY], ou...  70.7 us

profile of v4, /device:TPU:51, one launch (start us, length us, event | category | flops | bytes accessed | tf_op | source)
XLA Modules:
  0.0 258.4 jit_solution(17577325745429831938)
XLA Ops:
  0.0 70.7 %front.1 = (bf16[128,2048]{1,0:T(8,128)(2,1)}, bf16[256,2048]{1,0:T(8,128)(2,1)}, bf16[256,1536]{1,0:T(8,128)(2,1)}, f32[256,10]{1,0:T(8,128)}) custom-call(bf16[128,4096]{1,0:T(8,128)(2,1)} %mixed.1, f32[4,4096]{1,0:T(4,128)} %conv.1, f32[16,128]{1,0:T(8,128)} %bitcast.7, f32[16,128]{1,0:T(8,128)} %bitcast.8, s32[10,128]{1,0:T(8,128)} %bitcast.9, ...), custom_call_target="tpu_custom_call" | custom-call | flops 30000001024 | bytes 14000000 | tf_op jit(solution)/shard_map/front/pallas_call | solution.py:398
  70.7 185.8 %experts.1 = bf16[128,2048]{1,0:T(8,128)(2,1)} custom-call(bf16[256,2048]{1,0:T(8,128)(2,1)} %get-tuple-element.9.routed, bf16[128,2048]{1,0:T(8,128)(2,1)} %get-tuple-element.10.after, bf16[256,1536]{1,0:T(8,128)(2,1)} %get-tuple-element.11.sel, f32[256,10]{1,0:T(8,128)} %get-tuple-element.12.ids_ref, s32[8,1536]{1,0:T(8,128)} %constant.2.clone.table_ref, ...), custom_call_target="tpu_custom_call" | custom-call | flops 60000002048 | bytes 30000000 | tf_op jit(solution)/shard_map/experts/pallas_call | solution.py:650
  256.6 1.9 copy.21
